TPU v7x, 32 devices: a whole 2x2x4 slice. The times are simulated.
32 devices in a mesh: grp: 8 (over z, y), col: 4 (over x, core).
Axes of the slice: x: 2, y: 2, z: 4, core: 2. Of those that a mesh axis runs over, the one named last changes fastest.
Arguments:
- features: bfloat16 [65536, 256], P(('grp', 'col')), may hold values from -6 to 6
- adj_tiles: bfloat16 [1536, 256, 256], P('grp'), may hold values from 0 to 1.5
- block_pairs: int32 [8, 192, 2], P('grp'), may hold values from 0 to 31, as said below
- tile_count: int32 [8], P('grp'), may hold values from 32 to 192, as said below
- degree: int32 [65536], P('grp'), may hold values from 1 to 769
- labels: int32 [65536], P(('grp', 'col')), may hold values from 0 to 63
- loss_mask: int32 [65536], P(('grp', 'col')), may hold values from 0 to 1
- slot_piece: int32 [8, 79], replicated, may hold values from -1 to 416, as said below
- master: float32 [632, 2, 256], P('grp', None, 'col'), may hold values from -4 to 4
- moment_one: float32 [632, 2, 256], P('grp', None, 'col'), may hold values from -0.125 to 0.125
- moment_two: float32 [632, 2, 256], P('grp', None, 'col'), may hold values from 3.0517579e-06 to 0.00030517578
Outputs:
- mean_loss: float32 [], replicated
- new_master: float32 [632, 2, 256], P('grp', None, 'col')
- new_moment_one: float32 [632, 2, 256], P('grp', None, 'col')
- new_moment_two: float32 [632, 2, 256], P('grp', None, 'col')
- new_weights: bfloat16 [632, 2, 256], P('grp', None, 'col')
Inputs may be any that keep to these rules, and one draw needn't show every extreme that they name: `block_pairs`: of each group, the first tile_count entries are distinct pairs of blocks and include every diagonal pair (r, r); later entries are padding. `tile_count`: some group has 192 live tiles in every draw. `slot_piece`: each piece 0 to 416 sits in exactly one slot; a group holds at most 79 pieces, and some group holds 79 in every draw.
All inputs are finite; a program needn't handle non-finite values.
Results may differ from a plain program's by a relative error of at most 0.0079.
Values may be sent and summed in bfloat16 or wider, within the bound.
A program may use at most 128 MiB of HBM per device.

v0:
```python
import jax
import jax.numpy as jnp
from jax import lax
from jax.sharding import PartitionSpec as P

F = 256
HID = 256
CLS = 64
B = 256
PR = 2
STEP = 7
PROWS = 834
PIECES = 417


learn_rate = 0.01
beta_one = 0.5
beta_two = 0.5
adam_epsilon = 1e-08
decay_rate = 0.1


def contract_rows(left, right):
    return lax.dot_general(
        left, right, (((0,), (0,)), ((), ())), preferred_element_type=jnp.float32
    )


def contract_cols(left, right):
    return lax.dot_general(
        left, right, (((1,), (1,)), ((), ())), preferred_element_type=jnp.float32
    )


def body(
    features,
    adj_tiles,
    block_pairs,
    tile_count,
    degree,
    labels,
    loss_mask,
    slot_piece,
    master,
    moment_one,
    moment_two,
):
    col_count = lax.axis_size("col")
    grp_count = lax.axis_size("grp")
    col_index = lax.axis_index("col")
    grp_index = lax.axis_index("grp")
    node_rows = features.shape[0]
    group_nodes = degree.shape[0]
    block_count = group_nodes // B
    tile_slots = adj_tiles.shape[0]
    slot_width = slot_piece.shape[1]
    col_width = master.shape[2]
    own_slots = master.astype(jnp.bfloat16)[None]
    gathered = lax.all_gather(own_slots, ("grp", "col"), axis=0, tiled=True)
    slot_values = gathered.reshape(grp_count, col_count, slot_width, PR, col_width)
    slot_values = slot_values.transpose(0, 2, 3, 1, 4).reshape(
        grp_count * slot_width, PR, col_count * col_width
    )
    flat_slots = slot_piece.reshape(-1)
    positions = jnp.arange(flat_slots.shape[0], dtype=jnp.int32)
    target = jnp.where(flat_slots >= 0, flat_slots, PIECES)
    piece_slot = jnp.zeros((PIECES + 1,), jnp.int32).at[target].set(positions)[:PIECES]
    weight_table = slot_values[piece_slot].reshape(PROWS, HID)
    encoder_weight = weight_table[:F]
    self_weight = weight_table[F : F + HID]
    neigh_weight = weight_table[F + HID : F + 2 * HID]
    head_weight = weight_table[F + 2 * HID : F + 2 * HID + CLS]
    encoder_bias = weight_table[PROWS - 2].astype(jnp.float32)
    sage_bias = weight_table[PROWS - 1].astype(jnp.float32)
    mask_values = loss_mask.astype(jnp.float32)
    labelled = lax.psum(jnp.sum(mask_values), ("grp", "col"))
    preact = jnp.dot(features, encoder_weight, preferred_element_type=jnp.float32) + encoder_bias
    sig_pre = jax.nn.sigmoid(preact)
    encoded = (preact * sig_pre).astype(jnp.bfloat16)
    enc_columns = lax.all_to_all(encoded, "col", split_axis=1, concat_axis=0, tiled=True)
    pairs = block_pairs[0]
    row_blocks = pairs[:, 0]
    col_blocks = pairs[:, 1]
    live_tiles = jnp.arange(tile_slots, dtype=jnp.int32) < tile_count[0]
    block_ids = jnp.arange(block_count, dtype=jnp.int32)
    row_places = ((row_blocks[None, :] == block_ids[:, None]) & live_tiles[None, :]).astype(
        jnp.float32
    )
    picked = enc_columns.reshape(block_count, B, -1)[col_blocks]
    products = jnp.einsum("tij,tjc->tic", adj_tiles, picked, preferred_element_type=jnp.float32)
    block_sums = jnp.einsum("rt,tic->ric", row_places, products, precision=lax.Precision.HIGHEST)
    degree_values = degree.astype(jnp.float32)
    mean_columns = (block_sums.reshape(group_nodes, -1) / degree_values[:, None]).astype(
        jnp.bfloat16
    )
    neigh_mean = lax.all_to_all(mean_columns, "col", split_axis=0, concat_axis=1, tiled=True)
    sage_pre = (
        jnp.dot(encoded, self_weight, preferred_element_type=jnp.float32)
        + jnp.dot(neigh_mean, neigh_weight, preferred_element_type=jnp.float32)
        + sage_bias
    )
    sig_sage = jax.nn.sigmoid(sage_pre)
    hidden = (sage_pre * sig_sage).astype(jnp.bfloat16)
    logits = contract_cols(hidden, head_weight)
    row_max = jnp.max(logits, axis=1, keepdims=True)
    log_total = row_max[:, 0] + jnp.log(jnp.sum(jnp.exp(logits - row_max), axis=1))
    label_hot = (labels[:, None] == jnp.arange(CLS, dtype=jnp.int32)[None, :]).astype(jnp.float32)
    target_logit = jnp.sum(logits * label_hot, axis=1)
    local_loss = jnp.sum(mask_values * (log_total - target_logit))
    probability = jnp.exp(logits - log_total[:, None])
    logit_grad = ((probability - label_hot) * mask_values[:, None] / labelled).astype(jnp.bfloat16)
    head_grad = contract_rows(logit_grad, hidden)
    hidden_grad = jnp.dot(logit_grad, head_weight, preferred_element_type=jnp.float32)
    sage_grad = (hidden_grad * sig_sage * (1.0 + sage_pre * (1.0 - sig_sage))).astype(jnp.bfloat16)
    self_grad = contract_rows(encoded, sage_grad)
    neigh_grad = contract_rows(neigh_mean, sage_grad)
    sage_bias_grad = jnp.sum(sage_grad.astype(jnp.float32), axis=0)
    self_back = contract_cols(sage_grad, self_weight)
    neigh_back = contract_cols(sage_grad, neigh_weight)
    degree_rows = lax.dynamic_slice_in_dim(degree_values, col_index * node_rows, node_rows)
    sum_grad = (neigh_back / degree_rows[:, None]).astype(jnp.bfloat16)
    grad_columns = lax.all_to_all(sum_grad, "col", split_axis=1, concat_axis=0, tiled=True)
    picked_grad = grad_columns.reshape(block_count, B, -1)[row_blocks]
    back_products = jnp.einsum(
        "tij,tic->tjc", adj_tiles, picked_grad, preferred_element_type=jnp.float32
    )
    col_places = ((col_blocks[None, :] == block_ids[:, None]) & live_tiles[None, :]).astype(
        jnp.float32
    )
    back_blocks = jnp.einsum(
        "rt,tjc->rjc", col_places, back_products, precision=lax.Precision.HIGHEST
    )
    neigh_return = lax.all_to_all(
        back_blocks.reshape(group_nodes, -1).astype(jnp.bfloat16),
        "col",
        split_axis=0,
        concat_axis=1,
        tiled=True,
    ).astype(jnp.float32)
    encoded_grad = self_back + neigh_return
    preact_grad = (encoded_grad * sig_pre * (1.0 + preact * (1.0 - sig_pre))).astype(jnp.bfloat16)
    encoder_grad = contract_rows(features, preact_grad)
    encoder_bias_grad = jnp.sum(preact_grad.astype(jnp.float32), axis=0)
    grad_table = jnp.concatenate(
        [
            encoder_grad,
            self_grad,
            neigh_grad,
            head_grad,
            encoder_bias_grad[None, :],
            sage_bias_grad[None, :],
        ],
        axis=0,
    )
    loss_total = lax.psum(local_loss, ("grp", "col"))
    mean_loss = loss_total / labelled
    group_grad = lax.psum_scatter(
        grad_table.astype(jnp.bfloat16), "col", scatter_dimension=1, tiled=True
    ).astype(jnp.float32)
    my_pieces = lax.dynamic_slice_in_dim(slot_piece, grp_index, 1, 0)[0]
    is_owned = my_pieces >= 0
    safe_pieces = jnp.where(is_owned, my_pieces, 0)
    owned_values = is_owned[:, None, None]
    total_grad = lax.psum(group_grad, "grp")
    slot_grad = jnp.where(owned_values, total_grad.reshape(PIECES, PR, -1)[safe_pieces], 0.0)
    table_rows = safe_pieces[:, None] * PR + jnp.arange(PR, dtype=jnp.int32)[None, :]
    decay_values = jnp.where(table_rows < PROWS - 2, decay_rate, 0.0)[:, :, None]
    first_moment = beta_one * moment_one + (1.0 - beta_one) * slot_grad
    second_moment = beta_two * moment_two + (1.0 - beta_two) * slot_grad * slot_grad
    first_hat = first_moment / (1.0 - beta_one**STEP)
    second_hat = second_moment / (1.0 - beta_two**STEP)
    updated = master - learn_rate * (
        first_hat / (jnp.sqrt(second_hat) + adam_epsilon) + decay_values * master
    )
    updated = jnp.where(owned_values, updated, 0.0)
    first_moment = jnp.where(owned_values, first_moment, 0.0)
    second_moment = jnp.where(owned_values, second_moment, 0.0)
    return (mean_loss, updated, first_moment, second_moment, updated.astype(jnp.bfloat16))


def solution(mesh):
    in_specs = (
        P(("grp", "col"), None),
        P("grp", None, None),
        P("grp", None, None),
        P("grp"),
        P("grp"),
        P(("grp", "col")),
        P(("grp", "col")),
        P(),
        P("grp", None, "col"),
        P("grp", None, "col"),
        P("grp", None, "col"),
    )
    out_specs = (
        P(),
        P("grp", None, "col"),
        P("grp", None, "col"),
        P("grp", None, "col"),
        P("grp", None, "col"),
    )
    return jax.shard_map(body, mesh=mesh, in_specs=in_specs, out_specs=out_specs, check_vma=False)
```

profile of v0, /device:TPU:0, one launch (start us, length us, event | category | flops | bytes accessed | tf_op | source)
XLA Modules:
  0.0 409.5 jit_solution(9063719519104682953)
XLA Ops:
  8.2 46.8 %all-gather = bf16[2528,2,64]{2,1,0:T(2,128)(2,1)S(1)} all-gather(bf16[79,2,64]{2,1,0:T(2,128)(2,1)S(1)} %copy.83), channel_id=2, replica_groups=mesh['grp'=8,'col'=4] {'grp','col'}, dimensions={0}, use_global_device_ids=true | all-gather | bytes 667392 | tf_op jit(solution)/shard_map/all_gather | solution.py:59
  58.3 4.1 scatter_custom_fusion
  62.4 2.7 gather_fusion
  66.7 2.5 multiply_convert_fusion.1
  69.2 4.2 %all-to-all-start = ((bf16[2048,4,64]{0,2,1:T(8,128)(2,1)}), bf16[2048,4,64]{0,2,1:T(8,128)(2,1)S(1)}, u32[]{:S(2)}, u32[]{:S(2)}) async-start(bf16[2048,4,64]{0,2,1:T(8,128)(2,1)} %bitcast.8), calls=%async_computation | async-start | bytes 2097152 | tf_op jit(solution)/shard_map/all_to_all | solution.py:80
  74.2 13.6 %all-to-all-done = bf16[2048,4,64]{0,2,1:T(8,128)(2,1)S(1)} async-done(((bf16[2048,4,64]{0,2,1:T(8,128)(2,1)}), bf16[2048,4,64]{0,2,1:T(8,128)(2,1)S(1)}, u32[]{:S(2)}, u32[]{:S(2)}) %all-to-all-start) | async-done | bytes 1048608 | tf_op jit(solution)/shard_map/all_to_all | solution.py:80
  90.2 1.8 copy.87
  92.0 8.0 %gather_fusion.1 = bf16[192,256,64]{1,2,0:T(8,128)(2,1)} fusion(bf16[32,256,64]{1,2,0:T(8,128)(2,1)S(1)} %copy.87, s32[1024]{0:T(1024)S(1)} %pad_clamp_fusion.2), kind=kCustom, calls=%fused_computation.1 | custom fusion | bytes 12583680 | tf_op jit(solution)/shard_map/gather | solution.py:89
  100.0 18.3 %convolution_bitcast_fusion.1 = f32[192,256,64]{1,2,0:T(8,128)} fusion(bf16[192,256,64]{1,2,0:T(8,128)(2,1)} %gather_fusion.1, bf16[192,256,256]{2,1,0:T(8,128)(2,1)} %param.12), kind=kOutput, calls=%fused_computation.10 | convolution fusion | flops 1610612736 | bytes 44040192 | tf_op jit(solution)/shard_map/tij,tjc->tic/dot_general | solution.py:90
  118.3 16.5 %fusion.2 = f32[32,256,64]{1,0,2:T(8,128)} fusion(f32[192,256,64]{1,2,0:T(8,128)} %convolution_bitcast_fusion.1, s32[192]{0:T(256)S(1)} %bitcast.95, pred[192]{0:T(512)(128)(4,1)S(1)} %iota_compare_fusion.3), kind=kOutput, calls=%fused_computation.7 | convolution fusion | flops 1207971840 | bytes 14681024 | tf_op jit(solution)/shard_map/rt,tic->ric/dot_general | solution.py:91
  134.8 2.2 reshape.175
  137.0 2.1 fusion.12
  139.1 3.6 all-to-all-start.1
  143.0 3.0 fusion.40
  146.0 11.1 %all-to-all-done.1 = bf16[4,2048,64]{1,2,0:T(8,128)(2,1)S(1)} async-done(((bf16[4,2048,64]{1,2,0:T(8,128)(2,1)}), bf16[4,2048,64]{1,2,0:T(8,128)(2,1)S(1)}, u32[]{:S(2)}, u32[]{:S(2)}) %all-to-all-start.1) | async-done | bytes 1048608 | tf_op jit(solution)/shard_map/all_to_all | solution.py:96
  157.2 3.7 multiply_convert_fusion
  163.0 37.3 %all-reduce = (f32[]{:T(128)}, f32[]{:T(128)}) all-reduce(f32[]{:T(128)} %get-tuple-element.27, f32[]{:T(128)} %get-tuple-element.28), channel_id=1, replica_groups=mesh['grp'=8,'col'=4] {'grp','col'}, use_global_device_ids=true, to_apply=%region_7.8 | all-reduce | flops 2 | bytes 16 | tf_op jit(solution)/shard_map/psum | solution.py:76
  200.3 3.4 fusion.39
  205.1 3.5 all-to-all-start.2
  208.7 14.4 %all-to-all-done.2 = bf16[2048,4,64]{0,2,1:T(8,128)(2,1)S(1)} async-done(((bf16[2048,4,64]{0,2,1:T(8,128)(2,1)}), bf16[2048,4,64]{0,2,1:T(8,128)(2,1)S(1)}, u32[]{:S(2)}, u32[]{:S(2)}) %all-to-all-start.2) | async-done | bytes 1048608 | tf_op jit(solution)/shard_map/all_to_all | solution.py:122
  223.1 1.8 copy.94
  224.9 2.6 reshape.176
  227.5 1.8 copy.95
  229.3 8.0 %gather_fusion.2 = bf16[192,256,64]{1,2,0:T(8,128)(2,1)} fusion(bf16[32,256,64]{1,2,0:T(8,128)(2,1)S(1)} %copy.95, s32[1024]{0:T(1024)S(1)} %pad_clamp_fusion.1), kind=kCustom, calls=%fused_computation.2 | custom fusion | bytes 12583680 | tf_op jit(solution)/shard_map/gather | solution.py:123
  237.3 19.0 %convolution_bitcast_fusion = f32[192,256,64]{1,2,0:T(8,128)} fusion(bf16[192,256,64]{1,2,0:T(8,128)(2,1)} %gather_fusion.2, bf16[192,256,256]{2,1,0:T(8,128)(2,1)} %param.12), kind=kOutput, calls=%fused_computation.9 | convolution fusion | flops 1610612736 | bytes 44040192 | tf_op jit(solution)/shard_map/tij,tic->tjc/dot_general | solution.py:124
  256.3 16.5 %fusion.13 = bf16[32,256,64]{1,0,2:T(8,128)(2,1)} fusion(f32[192,256,64]{1,2,0:T(8,128)} %convolution_bitcast_fusion, s32[192]{0:T(256)S(1)} %bitcast.94, pred[192]{0:T(512)(128)(4,1)S(1)} %iota_compare_fusion.3), kind=kOutput, calls=%fused_computation.30 | convolution fusion | flops 1208496128 | bytes 13632448 | tf_op jit(solution)/shard_map/rt,tjc->rjc/dot_general | solution.py:130
  272.7 1.9 convert_element_type.80
  276.2 3.5 all-to-all-start.3
  279.7 3.2 convolution_convert_fusion.3
  285.1 9.0 %all-to-all-done.3 = bf16[4,2048,64]{1,2,0:T(8,128)(2,1)S(1)} async-done(((bf16[4,2048,64]{1,2,0:T(8,128)(2,1)}), bf16[4,2048,64]{1,2,0:T(8,128)(2,1)S(1)}, u32[]{:S(2)}, u32[]{:S(2)}) %all-to-all-start.3) | async-done | bytes 1048608 | tf_op jit(solution)/shard_map/all_to_all | solution.py:133
  299.1 21.4 %reduce-scatter.4.cloned.1.call-done = bf16[64,834]{1,0:T(8,128)(2,1)} async-done(((bf16[256,834]{1,0:T(8,128)(2,1)}), bf16[64,834]{1,0:T(8,128)(2,1)}) %reduce-scatter.4.cloned.1.call-update) | async-done | bytes 106768
  324.1 72.0 %all-reduce.3.cloned.1.call-done = f32[417,2,64]{2,1,0:T(2,128)} async-done(((f32[417,2,64]{2,1,0:T(2,128)}), f32[417,2,64]{2,1,0:T(2,128)}) %all-reduce.3.cloned.1.call-update) | async-done | bytes 213520 | tf_op jit(solution)/shard_map/psum | solution.py:164
  (102 shorter events, 27.9 us)
Async XLA Ops:
  7.2 59.5 %copy-start = (bf16[2048,256]{1,0:T(8,128)(2,1)S(1)}, bf16[2048,256]{1,0:T(8,128)(2,1)}, u32[]{:S(2)}) copy-start(bf16[2048,256]{1,0:T(8,128)(2,1)} %param.11) | copy-start | bytes 3145732
  55.0 3.2 copy-start.15
  65.1 4.1 %copy-start.4 = (bf16[417,2,256]{2,1,0:T(2,128)(2,1)}, bf16[417,2,256]{2,1,0:T(2,128)(2,1)S(1)}, u32[]{:S(2)}) copy-start(bf16[417,2,256]{2,1,0:T(2,128)(2,1)S(1)} %gather_fusion) | copy-start | bytes 1281028
  69.2 4.8 %copy-start.11 = (s32[8192]{0:T(1024)S(1)}, s32[8192]{0:T(1024)}, u32[]{:S(2)}) copy-start(s32[8192]{0:T(1024)} %param.15) | copy-start | bytes 98308
  69.2 4.9 %copy-start.16 = (s32[1,192,2]{1,2,0:T(2,128)S(1)}, s32[1,192,2]{1,2,0:T(2,128)}, u32[]{:S(2)}) copy-start(s32[1,192,2]{1,2,0:T(2,128)} %param.13) | copy-start | bytes 4612
  69.2 18.6 %all-to-all-start = ((bf16[2048,4,64]{0,2,1:T(8,128)(2,1)}), bf16[2048,4,64]{0,2,1:T(8,128)(2,1)S(1)}, u32[]{:S(2)}, u32[]{:S(2)}) async-start(bf16[2048,4,64]{0,2,1:T(8,128)(2,1)} %bitcast.8), calls=%async_computation | async-start | bytes 2097152 | tf_op jit(solution)/shard_map/all_to_all | solution.py:80
  74.1 13.7 %copy-start.8 = (f32[8192]{0:T(1024)}, f32[8192]{0:T(1024)S(1)}, u32[]{:S(2)}) copy-start(f32[8192]{0:T(1024)S(1)} %convert_element_type.72) | copy-start | bytes 98308
  139.1 3.8 slice-start
  139.1 3.8 copy-start.12
  139.1 18.1 %all-to-all-start.1 = ((bf16[4,2048,64]{1,2,0:T(8,128)(2,1)}), bf16[4,2048,64]{1,2,0:T(8,128)(2,1)S(1)}, u32[]{:S(2)}, u32[]{:S(2)}) async-start(bf16[4,2048,64]{1,2,0:T(8,128)(2,1)} %fusion.12), calls=%async_computation.1 | async-start | bytes 2097152 | tf_op jit(solution)/shard_map/all_to_all | solution.py:96
  142.8 14.4 %copy-start.17 = (f32[1,256]{1,0:T(1,128)S(1)}, f32[1,256]{1,0:T(1,128)}, u32[]{:S(2)}) copy-start(f32[1,256]{1,0:T(1,128)} %get-tuple-element.34) | copy-start | bytes 3076
  157.2 5.0 %copy-start.14 = (s32[2048]{0:T(1024)S(1)}, s32[2048]{0:T(1024)}, u32[]{:S(2)}) copy-start(s32[2048]{0:T(1024)} %param.16) | copy-start | bytes 24580
  160.9 1.0 copy-start.6
  162.2 41.5 %copy-start.5 = (f32[2048,64]{0,1:T(8,128)}, f32[2048,64]{0,1:T(8,128)S(1)}, u32[]{:S(2)}) copy-start(f32[2048,64]{0,1:T(8,128)S(1)} %get-tuple-element.50) | copy-start | bytes 1572868
  200.3 3.4 dynamic-slice-start
  203.7 1.5 copy-start.1
  205.1 18.0 %all-to-all-start.2 = ((bf16[2048,4,64]{0,2,1:T(8,128)(2,1)}), bf16[2048,4,64]{0,2,1:T(8,128)(2,1)S(1)}, u32[]{:S(2)}, u32[]{:S(2)}) async-start(bf16[2048,4,64]{0,2,1:T(8,128)(2,1)} %bitcast.92), calls=%async_computation.2 | async-start | bytes 2097152 | tf_op jit(solution)/shard_map/all_to_all | solution.py:122
  276.2 17.9 %all-to-all-start.3 = ((bf16[4,2048,64]{1,2,0:T(8,128)(2,1)}), bf16[4,2048,64]{1,2,0:T(8,128)(2,1)S(1)}, u32[]{:S(2)}, u32[]{:S(2)}) async-start(bf16[4,2048,64]{1,2,0:T(8,128)(2,1)} %copy.97), calls=%async_computation.3 | async-start | bytes 2097152 | tf_op jit(solution)/shard_map/all_to_all | solution.py:133
  279.7 40.9 %reduce-scatter.4.cloned.1.call-start = ((), (), s32[]{:S(2)}) async-start(), calls=%async_computation.6 | async-start | bytes 573440
  279.7 3.2 copy-start.2
  285.1 9.2 %copy-start.3 = (bf16[2048,256]{0,1:T(8,128)(2,1)S(1)}, bf16[2048,256]{0,1:T(8,128)(2,1)}, u32[]{:S(2)}) copy-start(bf16[2048,256]{0,1:T(8,128)(2,1)} %copy-done.1) | copy-start | bytes 3145732
  294.1 1.6 copy-start.18
  296.8 0.8 copy-start.13
  296.8 1.9 copy-start.7
  296.9 2.0 copy-start.9
  296.9 2.1 copy-start.10
  298.7 97.4 %all-reduce.3.cloned.1.call-start = ((), (), s32[]{:S(2)}) async-start(), calls=%async_computation.5 | async-start | bytes 854016 | tf_op jit(solution)/shard_map/psum | solution.py:164
Sparse Core Ops, SparseCore 0:
  298.8 21.7 reduce-scatter.3
  324.0 72.0 all-reduce.2
where the time goes:
time: 415 us; the launch traced here: 410 us
  waiting for transfers between devices  142 us (34%)
  matrix products  91.8 us (22%)
  blocking collectives  84 us (20%)
  local copies, waits for them, and re-layouts  53.8 us (13%)
  between operations  18.1 us (4%)
  starting transfers between devices  15 us (4%)
  other arithmetic  5.23 us (1%)
    psum x1, waiting for transfers between devices, body(): total_grad = lax.psum(group_grad, 'grp')  72 us
    all_gather x1, blocking collectives, body(): gathered = lax.all_gather(own_slots, ('grp', 'col'), axis=0, tiled=True)  46.8 us
    psum x1, blocking collectives, body(): labelled = lax.psum(jnp.sum(mask_values), ('grp', 'col'))  37.3 us
    unnamed x3, waiting for transfers between devices  21.5 us
    dot_general x1, matrix products, body(): jnp.einsum('tij,tic->tjc', adj_tiles, picked_grad, preferred_element_type...  19 us
    dot_general x1, matrix products, body(): jnp.einsum('tij,tjc->tic', adj_tiles, picked, preferred_element_type=jnp....  18.3 us
    dot_general x1, matrix products, body(): jnp.einsum('rt,tic->ric', row_places, products, precision=lax.Precision.H...  16.5 us
    dot_general x1, matrix products, body(): jnp.einsum('rt,tjc->rjc', col_places, back_products, precision=lax.Precis...  16.5 us
  transfers between devices with their start and end apart: 6, of which 6 were waited for; matrix products, arithmetic and copies ran while one was open for 2% of the time, Pallas kernels for 0%

commit v1 on v0

v1 whole, which is shorter than its diff:
```python
import functools
import jax
import jax.numpy as jnp
from jax import lax
from jax.experimental import pallas as pl
from jax.experimental.pallas import tpu as pltpu
from jax.sharding import PartitionSpec as P

F = 256
HID = 256
CLS = 64
B = 256
PR = 2
STEP = 7
PROWS = 834
TROWS = 848
HALF = 128
UNROLL = 8

learn_rate = 0.01
beta_one = 0.5
beta_two = 0.5
adam_epsilon = 1e-08
decay_rate = 0.1

f32 = jnp.float32
bf16 = jnp.bfloat16
MESH = pl.DeviceIdType.MESH
VM = pl.BlockSpec(memory_space=pltpu.VMEM)
SM = pl.BlockSpec(memory_space=pltpu.SMEM)
ANY = pl.BlockSpec(memory_space=pl.ANY)


def sds(shape, dtype):
    return jax.ShapeDtypeStruct(shape, dtype)


def dot_nn(a, b):
    return lax.dot_general(a, b, (((1,), (0,)), ((), ())), preferred_element_type=f32)


def dot_nt(a, b):
    return lax.dot_general(a, b, (((1,), (1,)), ((), ())), preferred_element_type=f32)


def dot_tn(a, b):
    return lax.dot_general(a, b, (((0,), (0,)), ((), ())), preferred_element_type=f32)


def column_of(rows16, row):
    pick = (lax.broadcasted_iota(jnp.int32, (16, HALF), 0) == row).astype(bf16)
    return dot_tn(rows16, pick)


def place():
    g = lax.axis_index("grp")
    q = lax.axis_index("col")
    k = q % 2
    x = q // 2
    partner = q + 1 - 2 * k
    across = q + 2 - 4 * x
    return g, q, k, x, partner, across


def sigmoid(v):
    return jax.nn.sigmoid(v)


def gather_kernel(
    ng,
    feat,
    wmsg,
    srow,
    labels,
    mask,
    pairs,
    tcount,
    fbuf,
    enc,
    table,
    wtrans,
    hot,
    marks,
    lists,
    pmsg,
    wbuf,
    prow,
    local_sem,
    core_sem,
    mark_sem,
    ws_core,
    ws_x,
    ws_send,
    ws_recv,
    wr_send,
    wr_recv,
    xs_send,
    xs_recv,
    rl_send,
    rl_recv,
):
    g, q, k, x, partner, across = place()
    rows = feat.shape[0]
    chunks = rows // B
    blocks = chunks
    sp = wmsg.shape[1]
    tiles = pairs.shape[1]
    tpad = lists.shape[1]

    load = pltpu.make_async_copy(feat, fbuf.at[q], local_sem)
    load.start()
    marks[x] = jnp.where(mask[...] > 0, labels[...], -1)

    barrier = pltpu.get_barrier_semaphore()
    pl.semaphore_signal(barrier, inc=1, device_id=(g, partner), device_id_type=MESH)
    pl.semaphore_signal(barrier, inc=1, device_id=(g, across), device_id_type=MESH)

    def greet(d, c):
        pl.semaphore_signal(barrier, inc=1, device_id=((g + d) % ng, q), device_id_type=MESH)
        return c

    lax.fori_loop(1, ng, greet, 0)
    pl.semaphore_wait(barrier, ng + 1)

    def remote(src, dst, send, recv, dev):
        return pltpu.make_async_remote_copy(
            src_ref=src, dst_ref=dst, send_sem=send, recv_sem=recv, device_id=dev, device_id_type=MESH
        )

    first = remote(wmsg, pmsg, ws_core.at[0], ws_core.at[1], (g, partner))
    first.start()
    mark_copy = remote(marks.at[x], marks.at[x], mark_sem.at[0], mark_sem.at[1], (g, across))
    mark_copy.start()
    load.wait()

    def cross(i):
        piece = fbuf.at[q, pl.ds(pl.multiple_of(i * B, B), B)]
        return remote(piece, piece, xs_send.at[i], xs_recv.at[i], (g, across))

    cross(0).start()
    share = remote(fbuf.at[q], fbuf.at[q], core_sem.at[0], core_sem.at[1], (g, partner))
    share.start()

    first.wait()
    wbuf[k, g, x] = wmsg[k] + pmsg[k]
    second = remote(wbuf.at[k, g, x], wbuf.at[k, g, x], ws_x.at[0], ws_x.at[1], (g, across))
    second.start()

    def cross_all(i, c):
        cross(i).start()
        return c

    lax.fori_loop(1, chunks, cross_all, 0)
    second.wait()

    def to_group(d):
        return remote(
            wbuf.at[k, g], wbuf.at[k, g], ws_send.at[d], ws_recv.at[d], ((g + d) % ng, q)
        )

    def from_group(d):
        src = (g + ng - d) % ng
        return remote(wbuf.at[k, src], wbuf.at[k, src], ws_send.at[d], ws_recv.at[d], (src, q))

    def hand_over(d):
        src = (g + ng - d) % ng
        return remote(
            wbuf.at[k, src], wbuf.at[k, src], wr_send.at[d], wr_recv.at[d], (g, partner)
        )

    def handed(d):
        src = (g + ng - d) % ng
        return remote(
            wbuf.at[1 - k, src], wbuf.at[1 - k, src], wr_send.at[d], wr_recv.at[d], (g, partner)
        )

    def send_group(d, c):
        to_group(d).start()
        return c

    lax.fori_loop(1, ng, send_group, 0)
    hand_over(0).start()

    shift = blocks.bit_length() - 1
    prow[...] = jnp.zeros_like(prow)
    pick = (
        lax.broadcasted_iota(jnp.int32, (8, 2), 0) == lax.broadcasted_iota(jnp.int32, (8, 2), 1)
    ).astype(bf16)
    prow[:, :tiles] = dot_nt(pick, pairs[0].astype(f32).astype(bf16))
    rvec = prow[0:1, :].astype(jnp.int32)
    cvec = prow[1:2, :].astype(jnp.int32)
    tvec = lax.broadcasted_iota(jnp.int32, (1, tpad), 1)
    live = tvec < tcount[0]

    def split(v):
        quarter = lax.shift_right_logical(v, shift)
        local = lax.shift_right_logical(quarter, 1) * blocks + (v & (blocks - 1))
        return (quarter & 1) == k, local

    fmine, frow = split(rvec)
    bmine, bcol = split(cvec)
    fmine = fmine & live
    bmine = bmine & live
    upto = (
        lax.broadcasted_iota(jnp.int32, (tpad, tpad), 0)
        <= lax.broadcasted_iota(jnp.int32, (tpad, tpad), 1)
    ).astype(bf16)
    order = lax.broadcasted_iota(jnp.int32, (tpad, tpad), 0)
    zero = jnp.zeros((1, tpad), jnp.int32)

    def compact(mine, one, two):
        flag = mine.astype(f32)
        seen = dot_nn(jnp.broadcast_to(flag, (8, tpad)).astype(bf16), upto)[0:1].astype(jnp.int32)
        spot = jnp.where(mine, seen - 1, -1)
        chosen = (order == spot).astype(f32).astype(bf16)
        values = jnp.concatenate([tvec, one, two, zero, zero, zero, zero, zero], axis=0)
        packed = dot_nt(values.astype(f32).astype(bf16), chosen).astype(jnp.int32)
        total = jnp.sum(flag, axis=1, keepdims=True).astype(jnp.int32)
        past = tvec >= total
        return packed[0:1], jnp.where(past, 2 * blocks, packed[1:2]), packed[2:3], zero + total

    ft, fr, fc, fn = compact(fmine, frow, cvec)
    bt, bc, br, bn = compact(bmine, bcol, rvec)
    lists[...] = jnp.concatenate([ft, fr, fc, bt, bc, br, fn, bn], axis=0)

    hot[...] = (
        (lax.broadcasted_iota(jnp.int32, hot.shape, 0) == srow[...]).astype(f32).astype(bf16)
    )

    def pass_on(d, c):
        from_group(d).wait_recv()
        hand_over(d).start()
        return c

    lax.fori_loop(1, ng, pass_on, 0)

    def take(d, c):
        handed(d).wait_recv()
        return c

    lax.fori_loop(0, ng, take, 0)

    left = wbuf[:, :, 0].reshape(2 * ng * sp, HALF)
    right = wbuf[:, :, 1].reshape(2 * ng * sp, HALF)
    full = dot_nn(hot[...], jnp.concatenate([left, right], axis=1))
    table[...] = full.astype(bf16)
    for i in range(3):
        wtrans[i] = jnp.transpose(full[i * B : (i + 1) * B]).astype(bf16)
    bias = column_of(table[PROWS - 2 : PROWS + 14], 0)
    bias = jnp.concatenate([bias, bias], axis=1)

    def encode(quarter, i):
        piece = fbuf[quarter, pl.ds(pl.multiple_of(i * B, B), B)]
        pre = dot_nt(wtrans[0], piece) + bias
        enc[quarter * blocks + i] = (pre * sigmoid(pre)).astype(bf16)

    def own(i, c):
        encode(q, i)
        return c

    lax.fori_loop(0, blocks, own, 0)
    share.wait_recv()

    def near(i, c):
        encode(partner, i)
        return c

    lax.fori_loop(0, blocks, near, 0)
    mine_far = across
    near_far = partner + 2 - 4 * x

    def crossed(i):
        piece = fbuf.at[mine_far, pl.ds(pl.multiple_of(i * B, B), B)]
        return remote(piece, piece, xs_send.at[i], xs_recv.at[i], (g, across))

    def relay(i):
        piece = fbuf.at[mine_far, pl.ds(pl.multiple_of(i * B, B), B)]
        return remote(piece, piece, rl_send.at[i], rl_recv.at[i], (g, partner))

    def relayed(i):
        piece = fbuf.at[near_far, pl.ds(pl.multiple_of(i * B, B), B)]
        return remote(piece, piece, rl_send.at[i], rl_recv.at[i], (g, partner))

    def far(i, c):
        crossed(i).wait_recv()
        relay(i).start()
        encode(mine_far, i)

        @pl.when(i > 0)
        def _():
            relayed(i - 1).wait_recv()
            encode(near_far, i - 1)

        return c

    lax.fori_loop(0, chunks, far, 0)
    relayed(chunks - 1).wait_recv()
    encode(near_far, chunks - 1)

    mark_copy.wait()
    share.wait_send()

    def drain(i, c):
        cross(i).wait_send()
        relay(i).wait_send()
        return c

    lax.fori_loop(0, chunks, drain, 0)

    def drain_group(d, c):
        to_group(d).wait_send()
        hand_over(d).wait_send()
        return c

    lax.fori_loop(1, ng, drain_group, 0)
    hand_over(0).wait_send()


def forward_kernel(lists, tiles, enc, degree, mean, acc):
    k = lax.axis_index("col") % 2
    local = mean.shape[0]
    blocks = local // 2

    def clear(i, c):
        acc[i] = jnp.zeros((B, B), f32)
        return c

    lax.fori_loop(0, local + 1, clear, 0)
    count = lists[6, 0]

    def step(i, c):
        for u in range(UNROLL):
            j = i * UNROLL + u
            r = lists[1, j]
            acc[r] += dot_nt(enc[lists[2, j]], tiles[lists[0, j]])
        return c

    lax.fori_loop(0, (count + UNROLL - 1) // UNROLL, step, 0)

    def finish(i, c):
        scale = 1.0 / degree[(i // blocks) * 2 + k, :, pl.ds(pl.multiple_of((i % blocks) * B, B), B)].astype(f32)
        mean[i] = (acc[i] * scale).astype(bf16)
        return c

    lax.fori_loop(0, local, finish, 0)


def sage_kernel(
    enc,
    mean,
    table,
    wtrans,
    marks,
    degree,
    sums,
    self_back,
    self_grad,
    neigh_grad,
    head_grad,
    bias_grad,
    stats,
    sage,
    hid,
    lgrad,
    send,
    recv,
):
    g, q, k, x, partner, across = place()
    local = mean.shape[0]
    blocks = local // 2
    width = 2 * B
    steps = local // 2
    barrier = pltpu.get_barrier_semaphore()
    pl.semaphore_signal(barrier, inc=1, device_id=(g, partner), device_id_type=MESH)
    pl.semaphore_wait(barrier, 1)
    half = pl.ds(pl.multiple_of(x * HALF, HALF), HALF)
    head = table[F + 2 * HID : F + 2 * HID + CLS]
    bias = column_of(table[PROWS - 2 : PROWS + 14], 1)
    bias = jnp.concatenate([bias] * 4, axis=1)
    neigh_half = table[pl.ds(pl.multiple_of(F + HID + x * HALF, HALF), HALF)]
    self_half = table[pl.ds(pl.multiple_of(F + x * HALF, HALF), HALF)]
    stats[...] = jnp.zeros_like(stats)

    def slot(i, core):
        return (i // (steps // 2)) * 2 * blocks + core * blocks + (i % (steps // 2)) * 2

    def exchange(i, core):
        piece = sums.at[pl.ds(slot(i, core), 2)]
        return pltpu.make_async_remote_copy(
            src_ref=piece,
            dst_ref=piece,
            send_sem=send.at[i],
            recv_sem=recv.at[i],
            device_id=(g, partner),
            device_id_type=MESH,
        )

    def step(i, c):
        at = slot(i, k)
        e = jnp.concatenate([enc[at], enc[at + 1]], axis=1)
        m = jnp.concatenate([mean[2 * i], mean[2 * i + 1]], axis=1)
        pre = dot_nn(wtrans[1], e) + dot_nn(wtrans[2], m) + bias
        sig = sigmoid(pre)
        hidden = (pre * sig).astype(bf16)
        logits = dot_nn(head, hidden)
        top = jnp.max(logits, axis=0, keepdims=True)
        expd = jnp.exp(logits - top)
        total = jnp.sum(expd, axis=0, keepdims=True)
        cols = pl.ds(pl.multiple_of((i % (steps // 2)) * width, width), width)
        mark = marks[i // (steps // 2), :, cols]
        valid = (mark >= 0).astype(f32)
        onehot = (lax.broadcasted_iota(jnp.int32, (CLS, width), 0) == mark).astype(f32)
        target = jnp.sum(logits * onehot, axis=0, keepdims=True)
        loss = valid * (top + jnp.log(total) - target)
        stats[0:1, :] += loss
        stats[1:2, :] += valid
        grad = ((expd * (1.0 / total) - onehot) * valid).astype(bf16)
        back = dot_tn(head, grad) * (sig * (1.0 + pre * (1.0 - sig)))
        sgrad = back.astype(bf16)
        scale = 1.0 / degree[(i // (steps // 2)) * 2 + k, :, cols].astype(f32)
        out = (dot_nn(neigh_half, sgrad) * scale).astype(bf16)
        for b in range(2):
            lanes = slice(b * B, (b + 1) * B)
            sums[at + b] = out[:, lanes]
            sage[2 * i + b] = sgrad[:, lanes]
            hid[2 * i + b] = hidden[:, lanes]
            lgrad[2 * i + b] = grad[:, lanes]
        exchange(i, k).start()
        return c

    lax.fori_loop(0, steps, step, 0)

    ones = jnp.ones((B, HALF), bf16)
    sg = ng_ = hg = bg = None
    for b in range(local):
        at = (b // blocks) * 2 * blocks + k * blocks + b % blocks
        s = sage[b, half]
        t1 = dot_nt(s, enc[at])
        t2 = dot_nt(s, mean[b])
        t3 = dot_nt(lgrad[b], hid[b, half])
        t4 = dot_nn(s, ones)
        sg = t1 if sg is None else sg + t1
        ng_ = t2 if ng_ is None else ng_ + t2
        hg = t3 if hg is None else hg + t3
        bg = t4 if bg is None else bg + t4
        self_back[b] = dot_nn(self_half, sage[b])
    self_grad[...] = sg
    neigh_grad[...] = ng_
    head_grad[...] = hg
    bias_grad[...] = bg

    def done(i, c):
        exchange(i, 1 - k).wait_recv()
        exchange(i, k).wait_send()
        return c

    lax.fori_loop(0, steps, done, 0)


def backward_kernel(lists, tiles, sums, self_back, fbuf, table, wtrans, enc_grad, bias_grad, acc):
    q = lax.axis_index("col")
    k = q % 2
    x = q // 2
    local = self_back.shape[0]
    blocks = local // 2

    def clear(i, c):
        acc[i] = jnp.zeros((HALF, B), f32)
        return c

    lax.fori_loop(0, local + 1, clear, 0)
    count = lists[7, 0]

    def step(i, c):
        for u in range(UNROLL):
            j = i * UNROLL + u
            acc[lists[4, j]] += dot_nn(sums[lists[5, j]], tiles[lists[3, j]])
        return c

    lax.fori_loop(0, (count + UNROLL - 1) // UNROLL, step, 0)

    half = pl.ds(pl.multiple_of(x * HALF, HALF), HALF)
    wide = column_of(table[PROWS - 2 : PROWS + 14, half], 0)
    wide = jnp.concatenate([wide, wide], axis=1)
    weight = wtrans[0, half]
    eg = bg = None
    for b in range(local):
        piece = fbuf[(b // blocks) * 2 + k, (b % blocks) * B : (b % blocks + 1) * B]
        pre = dot_nt(weight, piece) + wide
        sig = sigmoid(pre)
        grad = ((self_back[b] + acc[b]) * (sig * (1.0 + pre * (1.0 - sig)))).astype(bf16)
        t1 = dot_nn(grad, piece)
        gf = grad.astype(f32)
        t2 = gf[:, :HALF] + gf[:, HALF:]
        eg = t1 if eg is None else eg + t1
        bg = t2 if bg is None else bg + t2
    enc_grad[...] = eg
    bias_grad[...] = bg


def reduce_kernel(
    ng,
    enc_grad,
    benc_grad,
    self_grad,
    neigh_grad,
    head_grad,
    bsage_grad,
    hot,
    stats,
    slot_grad,
    loss,
    gtab,
    pbuf,
    rbuf,
    qbuf,
    inbox,
    sbuf,
    srecv,
    sbox,
    core_sem,
    stat_sem,
    g_send,
    g_recv,
    s_send,
    s_recv,
):
    g, q, k, x, partner, across = place()
    barrier = pltpu.get_barrier_semaphore()
    pl.semaphore_signal(barrier, inc=1, device_id=(g, partner), device_id_type=MESH)

    def greet(d, c):
        pl.semaphore_signal(barrier, inc=1, device_id=((g + d) % ng, q), device_id_type=MESH)
        return c

    lax.fori_loop(1, ng, greet, 0)
    sp = inbox.shape[1]
    slots = ng * sp

    both = jnp.sum(stats[...], axis=1, keepdims=True)
    sbuf[...] = jnp.broadcast_to(both, sbuf.shape)
    gtab[0:B] = jnp.transpose(enc_grad[...])
    gtab[B : 2 * B] = jnp.transpose(self_grad[...])
    gtab[2 * B : 3 * B] = jnp.transpose(neigh_grad[...])
    gtab[3 * B : 3 * B + CLS] = head_grad[...]
    tail = lax.broadcasted_iota(jnp.int32, (16, HALF), 0)
    row_one = jnp.sum(jnp.transpose(benc_grad[...]), axis=0, keepdims=True)
    row_two = jnp.transpose(bsage_grad[...])[0:1]
    gtab[PROWS - 2 : PROWS + 14] = jnp.where(tail == 0, row_one, jnp.where(tail == 1, row_two, 0.0))
    whole = gtab[...]
    rolled = pltpu.roll(whole, HALF // 2, 1)
    low = lax.broadcasted_iota(jnp.int32, (TROWS, HALF), 1) < HALF // 2

    def spread(first, second):
        one = jnp.where(low, first, 0.0).astype(bf16)
        two = jnp.where(low, 0.0, second).astype(bf16)
        both = dot_tn(hot[:, :slots], one) + dot_tn(hot[:, slots:], two)
        return both.astype(bf16)

    pbuf[0] = spread(whole, rolled)
    pbuf[1] = spread(rolled, whole)
    pl.semaphore_wait(barrier, ng)

    def remote(src, dst, send, recv, dev):
        return pltpu.make_async_remote_copy(
            src_ref=src, dst_ref=dst, send_sem=send, recv_sem=recv, device_id=dev, device_id_type=MESH
        )

    one = remote(pbuf.at[1 - k], rbuf, core_sem.at[0], core_sem.at[1], (g, partner))
    one.start()
    two = remote(sbuf, srecv, stat_sem.at[0], stat_sem.at[1], (g, partner))
    two.start()
    one.wait()
    two.wait()
    qbuf[...] = (
        (pbuf[k].astype(f32) + rbuf[...].astype(f32)).astype(bf16).reshape(ng, sp, HALF)
    )
    sbox[g] = sbuf[...] + srecv[...]

    def out(d):
        to = (g + d) % ng
        return remote(qbuf.at[to], inbox.at[g], g_send.at[d], g_recv.at[d], (to, q))

    def got(d):
        src = (g + ng - d) % ng
        return remote(qbuf.at[src], inbox.at[src], g_send.at[d], g_recv.at[d], (src, q))

    def stat_out(d):
        to = (g + d) % ng
        return remote(sbox.at[g], sbox.at[g], s_send.at[d], s_recv.at[d], (to, q))

    def stat_got(d):
        src = (g + ng - d) % ng
        return remote(sbox.at[src], sbox.at[src], s_send.at[d], s_recv.at[d], (src, q))

    def start(d, c):
        stat_out(d).start()
        out(d).start()
        return c

    lax.fori_loop(1, ng, start, 0)
    inbox[g] = qbuf[g]

    def arrive(d, c):
        stat_got(d).wait_recv()
        got(d).wait_recv()
        return c

    lax.fori_loop(1, ng, arrive, 0)

    def add_stat(i, c):
        return c + sbox[i]

    sums = lax.fori_loop(0, ng, add_stat, jnp.zeros(sbuf.shape, f32))
    loss_sum = sums[0:1]
    count = sums[1:2]
    loss[...] = jnp.broadcast_to(loss_sum / count, loss.shape)

    def add(i, c):
        return c + inbox[i].astype(f32)

    total = lax.fori_loop(0, ng, add, jnp.zeros((sp, HALF), f32))
    slot_grad[...] = total / count

    def finish(d, c):
        stat_out(d).wait_send()
        out(d).wait_send()
        return c

    lax.fori_loop(1, ng, finish, 0)


def params(limit, collective=None):
    return pltpu.CompilerParams(
        vmem_limit_bytes=limit << 20, collective_id=collective, has_side_effects=collective is not None
    )


DMA = pltpu.SemaphoreType.DMA


def body(
    features,
    adj_tiles,
    block_pairs,
    tile_count,
    degree,
    labels,
    loss_mask,
    slot_piece,
    master,
    moment_one,
    moment_two,
):
    nc = lax.axis_size("col")
    ng = lax.axis_size("grp")
    q = lax.axis_index("col")
    grp_index = lax.axis_index("grp")
    rows = features.shape[0]
    blocks = rows // B
    nb = nc * blocks
    local = 2 * blocks
    tile_slots = adj_tiles.shape[0]
    tpad = -(-tile_slots // HALF) * HALF
    slots = slot_piece.shape[1]
    sp = -(-slots // 16) * 16
    width = master.shape[2]
    chunks = blocks

    flat = jnp.transpose(master.astype(bf16), (1, 0, 2))
    flat = jnp.pad(flat, ((0, 0), (0, sp - slots), (0, 0)))
    empty = jnp.zeros_like(flat)
    wmsg = jnp.where(
        q % 2 == 0,
        jnp.concatenate([flat, empty], axis=2),
        jnp.concatenate([empty, flat], axis=2),
    )
    piece = jnp.pad(slot_piece, ((0, 0), (0, sp - slots)), constant_values=-1).reshape(1, -1)
    srow = jnp.concatenate(
        [jnp.where(piece >= 0, piece * PR + j, -1) for j in range(PR)], axis=1
    )
    degree_rows = degree.reshape(nc, 1, rows)

    fbuf, enc, table, wtrans, hot, marks, lists = pl.pallas_call(
        functools.partial(gather_kernel, ng),
        out_shape=(
            sds((nc, rows, F), bf16),
            sds((nb, HID, B), bf16),
            sds((TROWS, HID), bf16),
            sds((3, HID, HID), bf16),
            sds((TROWS, 2 * ng * sp), bf16),
            sds((2, 1, rows), jnp.int32),
            sds((8, tpad), jnp.int32),
        ),
        in_specs=[ANY, VM, VM, VM, VM, VM, SM],
        out_specs=(VM,) * 7,
        scratch_shapes=[
            pltpu.VMEM((2, sp, HALF), bf16),
            pltpu.VMEM((2, ng, 2, sp, HALF), bf16),
            pltpu.VMEM((8, tpad), f32),
            DMA,
            DMA((2,)),
            DMA((2,)),
            DMA((2,)),
            DMA((2,)),
            DMA((ng,)),
            DMA((ng,)),
            DMA((ng,)),
            DMA((ng,)),
            DMA((chunks,)),
            DMA((chunks,)),
            DMA((chunks,)),
            DMA((chunks,)),
        ],
        compiler_params=params(24, 0),
        name="gather",
    )(
        features,
        wmsg,
        srow,
        labels.reshape(1, rows),
        loss_mask.reshape(1, rows),
        block_pairs,
        tile_count,
    )

    mean = pl.pallas_call(
        forward_kernel,
        out_shape=sds((local, HID, B), bf16),
        in_specs=[SM, VM, VM, VM],
        out_specs=VM,
        scratch_shapes=[pltpu.VMEM((local + 1, HID, B), f32)],
        compiler_params=params(56),
        name="forward",
    )(lists, adj_tiles, enc, degree_rows)

    sums, self_back, self_grad, neigh_grad, head_grad, bsage, stats = pl.pallas_call(
        sage_kernel,
        out_shape=(
            sds((nb, HALF, B), bf16),
            sds((local, HALF, B), f32),
            sds((HALF, HID), f32),
            sds((HALF, HID), f32),
            sds((CLS, HALF), f32),
            sds((HALF, HALF), f32),
            sds((8, 2 * B), f32),
        ),
        in_specs=[VM] * 6,
        out_specs=(VM,) * 7,
        scratch_shapes=[
            pltpu.VMEM((local, HID, B), bf16),
            pltpu.VMEM((local, HID, B), bf16),
            pltpu.VMEM((local, CLS, B), bf16),
            DMA((blocks,)),
            DMA((blocks,)),
        ],
        compiler_params=params(24, 1),
        name="sage",
    )(enc, mean, table, wtrans, marks, degree_rows)

    enc_grad, benc = pl.pallas_call(
        backward_kernel,
        out_shape=(sds((HALF, F), f32), sds((HALF, HALF), f32)),
        in_specs=[SM, VM, VM, VM, VM, VM, VM],
        out_specs=(VM,) * 2,
        scratch_shapes=[pltpu.VMEM((local + 1, HALF, B), f32)],
        compiler_params=params(56),
        name="backward",
    )(lists, adj_tiles, sums, self_back, fbuf, table, wtrans)

    packed, loss = pl.pallas_call(
        functools.partial(reduce_kernel, ng),
        out_shape=(sds((sp, HALF), f32), sds((8, HALF), f32)),
        in_specs=[VM] * 8,
        out_specs=(VM,) * 2,
        scratch_shapes=[
            pltpu.VMEM((TROWS, HALF), f32),
            pltpu.VMEM((2, ng * sp, HALF), bf16),
            pltpu.VMEM((ng * sp, HALF), bf16),
            pltpu.VMEM((ng, sp, HALF), bf16),
            pltpu.VMEM((ng, sp, HALF), bf16),
            pltpu.VMEM((8, HALF), f32),
            pltpu.VMEM((8, HALF), f32),
            pltpu.VMEM((ng, 8, HALF), f32),
            DMA((2,)),
            DMA((2,)),
            DMA((ng,)),
            DMA((ng,)),
            DMA((ng,)),
            DMA((ng,)),
        ],
        compiler_params=params(24, 2),
        name="reduce",
    )(enc_grad, benc, self_grad, neigh_grad, head_grad, bsage, hot, stats)

    mean_loss = loss[0, 0]
    my_pieces = lax.dynamic_slice_in_dim(slot_piece, grp_index, 1, 0)[0]
    is_owned = my_pieces >= 0
    safe_pieces = jnp.where(is_owned, my_pieces, 0)
    owned_values = is_owned[:, None, None]
    slot_grad = jnp.where(owned_values, packed[:slots].reshape(slots, PR, width), 0.0)
    table_rows = safe_pieces[:, None] * PR + jnp.arange(PR, dtype=jnp.int32)[None, :]
    decay_values = jnp.where(table_rows < PROWS - 2, decay_rate, 0.0)[:, :, None]
    first_moment = beta_one * moment_one + (1.0 - beta_one) * slot_grad
    second_moment = beta_two * moment_two + (1.0 - beta_two) * slot_grad * slot_grad
    first_hat = first_moment / (1.0 - beta_one**STEP)
    second_hat = second_moment / (1.0 - beta_two**STEP)
    updated = master - learn_rate * (
        first_hat / (jnp.sqrt(second_hat) + adam_epsilon) + decay_values * master
    )
    updated = jnp.where(owned_values, updated, 0.0)
    first_moment = jnp.where(owned_values, first_moment, 0.0)
    second_moment = jnp.where(owned_values, second_moment, 0.0)
    return (mean_loss, updated, first_moment, second_moment, updated.astype(jnp.bfloat16))


def solution(mesh):
    in_specs = (
        P(("grp", "col"), None),
        P("grp", None, None),
        P("grp", None, None),
        P("grp"),
        P("grp"),
        P(("grp", "col")),
        P(("grp", "col")),
        P(),
        P("grp", None, "col"),
        P("grp", None, "col"),
        P("grp", None, "col"),
    )
    out_specs = (
        P(),
        P("grp", None, "col"),
        P("grp", None, "col"),
        P("grp", None, "col"),
        P("grp", None, "col"),
    )
    return jax.shard_map(body, mesh=mesh, in_specs=in_specs, out_specs=out_specs, check_vma=False)
```

time: 415 us -> 111 us (0.27); the launches traced: 410 us -> 111 us
  waiting for transfers between devices: 142 us -> 0 us
  matrix products: 91.8 us -> 0 us
  Pallas kernels: 0 us -> 86.7 us
  blocking collectives: 84 us -> 0 us
  local copies, waits for them, and re-layouts: 53.8 us -> 18.1 us
  between operations: 18.1 us -> 1.46 us
  starting transfers between devices: 15 us -> 0 us
    dot_general x15 -> x0, matrix products: 91.8 us -> none  [the longest x1 19 us: body(): jnp.einsum('tij,tic->tjc', adj_tiles, picked_grad, preferred_element_type...]
    pallas_call x0 -> x5, Pallas kernels: none -> 86.7 us  [the longest x1 32.8 us: body(): pl.pallas_call(functools.partial(gather_kernel, ng), out_shape=(sds((nc,...]
    psum x1 -> x0, waiting for transfers between devices: 72 us -> none  [body(): total_grad = lax.psum(group_grad, 'grp')]
    all_to_all x4 -> x0, waiting for transfers between devices: 48.1 us -> none  [the longest x1 14.4 us: body(): lax.all_to_all(sum_grad, 'col', split_axis=1, concat_axis=0, tiled=True)]
    all_gather x1 -> x0, blocking collectives: 46.8 us -> none  [body(): gathered = lax.all_gather(own_slots, ('grp', 'col'), axis=0, tiled=True)]
    psum x1 -> x0, blocking collectives: 37.3 us -> none  [body(): labelled = lax.psum(jnp.sum(mask_values), ('grp', 'col'))]
    unnamed x3 -> x0, waiting for transfers between devices: 21.5 us -> none
    gather x4 -> x0, local copies, waits for them, and re-layouts: 20.3 us -> none  [the longest x1 7.99 us: body(): picked = enc_columns.reshape(block_count, B, -1)[col_blocks]]
  transfers between devices with their start and end apart: 6 -> 0, of which waited for: 6 -> 0; matrix products, arithmetic and copies ran while one was open for 2% -> 0% of each run, Pallas kernels for 0% -> 0%
where the time goes in v1:
time: 111 us
  Pallas kernels  86.7 us (78%)
  local copies, waits for them, and re-layouts  18.1 us (16%)
  other arithmetic  4.26 us (4%)
  between operations  1.46 us (1%)
    pallas_call x1, Pallas kernels, body(): pl.pallas_call(functools.partial(gather_kernel, ng), out_shape=(sds((nc,...  32.8 us
    pallas_call x1, Pallas kernels, body(): pl.pallas_call(forward_kernel, out_shape=sds((local, HID, B), bf16), in_s...  17.6 us
    unnamed x44, local copies, waits for them, and re-layouts  17.2 us
    pallas_call x1, Pallas kernels, body(): pl.pallas_call(backward_kernel, out_shape=(sds((HALF, F), f32), sds((HALF...  16.8 us
    pallas_call x1, Pallas kernels, body(): pl.pallas_call(sage_kernel, out_shape=(sds((nb, HALF, B), bf16), sds((loc...  10.1 us
    pallas_call x1, Pallas kernels, body(): pl.pallas_call(functools.partial(reduce_kernel, ng), out_shape=(sds((sp,...  9.45 us

profile of v1, /device:TPU:0, one launch (start us, length us, event | category | flops | bytes accessed | tf_op | source)
XLA Modules:
  0.0 110.6 jit_solution(16489877202250534360)
XLA Ops:
  0.6 0.8 convert_element_type.8
  1.5 0.1 copy.29
  1.7 0.7 pad_multiply_fusion
  2.5 0.7 pad_compare_fusion
  3.3 0.8 copy.30.pairs
  4.8 1.2 %copy-done.8 = bf16[2048,256]{1,0:T(8,128)(2,1)S(1)} copy-done((bf16[2048,256]{1,0:T(8,128)(2,1)S(1)}, bf16[2048,256]{1,0:T(8,128)(2,1)}, u32[]{:S(2)}) %copy-start.8) | copy-done | bytes 1048600
  6.0 0.7 copy-done.13
  6.7 0.7 copy-done.14
  7.4 32.8 %gather.1 = (bf16[4,2048,256]{2,1,0:T(8,128)(2,1)S(1)}, bf16[32,256,256]{2,1,0:T(8,128)(2,1)S(1)}, bf16[848,256]{1,0:T(8,128)(2,1)S(1)}, bf16[3,256,256]{2,1,0:T...) custom-call(bf16[2048,256]{1,0:T(8,128)(2,1)S(1)} %copy-done.8, ...), custom_call_target="tpu_custom_call" | custom-call | tf_op jit(solution)/shard_map/gather/pallas_call | solution.py:684
  40.2 2.0 %copy-done = bf16[32,256,256]{2,1,0:T(8,128)(2,1)} copy-done((bf16[32,256,256]{2,1,0:T(8,128)(2,1)}, bf16[32,256,256]{2,1,0:T(8,128)(2,1)S(1)}, u32[]{:S(2)}) %copy-start) | copy-done | bytes 4194328
  42.2 1.9 %copy-done.3 = bf16[4,2048,256]{2,1,0:T(8,128)(2,1)} copy-done((bf16[4,2048,256]{2,1,0:T(8,128)(2,1)}, bf16[4,2048,256]{2,1,0:T(8,128)(2,1)S(1)}, u32[]{:S(2)}) %copy-start.3) | copy-done | bytes 4194328
  44.1 0.6 copy-done.12
  44.7 17.6 %forward.1.mean = bf16[16,256,256]{2,1,0:T(8,128)(2,1)} custom-call(s32[8,256]{1,0:T(8,128)} %copy-done.12, bf16[192,256,256]{2,1,0:T(8,128)(2,1)} %tiles.3, bf16[32,256,256]{2,1,0:T(8,128)(2,1)} %copy-done, s32[4,1,2048]{2,1,0:T(1,128)} %bitcast.13), custom_call_target="tpu_custom_call" | custom-call | tf_op jit(solution)/shard_map/forward/pallas_call | solution.py:727
  62.4 1.6 %copy-done.2 = bf16[16,256,256]{2,1,0:T(8,128)(2,1)S(1)} copy-done((bf16[16,256,256]{2,1,0:T(8,128)(2,1)S(1)}, bf16[16,256,256]{2,1,0:T(8,128)(2,1)}, u32[]{:S(2)}) %copy-start.2) | copy-done | bytes 2097176
  64.0 10.1 %sage.1 = (bf16[32,128,256]{2,1,0:T(8,128)(2,1)S(1)}, f32[16,128,256]{2,1,0:T(8,128)S(1)}, f32[128,256]{1,0:T(8,128)S(1)}, f32[128,256]{1,0:T(8,128)S(1)}, f32[6...) custom-call(bf16[32,256,256]{2,1,0:T(8,128)(2,1)S(1)} %copy-done.1, ...), custom_call_target="tpu_custom_call" | custom-call | tf_op jit(solution)/shard_map/sage/pallas_call | solution.py:737
  74.1 1.3 %copy-done.4 = bf16[32,128,256]{2,1,0:T(8,128)(2,1)} copy-done((bf16[32,128,256]{2,1,0:T(8,128)(2,1)}, bf16[32,128,256]{2,1,0:T(8,128)(2,1)S(1)}, u32[]{:S(2)}) %copy-start.4) | copy-done | bytes 2097176
  75.4 1.4 %copy-done.5 = f32[16,128,256]{2,1,0:T(8,128)} copy-done((f32[16,128,256]{2,1,0:T(8,128)}, f32[16,128,256]{2,1,0:T(8,128)S(1)}, u32[]{:S(2)}) %copy-start.5) | copy-done | bytes 2097176
  76.8 16.8 %backward.1 = (f32[128,256]{1,0:T(8,128)}, f32[128,128]{1,0:T(8,128)}) custom-call(s32[8,256]{1,0:T(8,128)} %copy-done.12, bf16[192,256,256]{2,1,0:T(8,128)(2,1)} %tiles.3, bf16[32,128,256]{2,1,0:T(8,128)(2,1)} %copy-done.4, f32[16,128,256]{2,1,0:T(8,128)} %copy-done.5, bf16[4,2048,256]{2,1,0:T(8,128)(2,1)} %copy-done.3, bf16[848,256]{1,0:T(8,128)(2,1)} %copy-done.6, ...), custom_call_target="tpu_custom_call" | custom-call | tf_op jit(solution)/shard_map/backward/pallas_call | solution.py:761
  93.6 0.9 copy-done.10
  94.5 0.8 copy-done.11
  95.3 9.5 %reduce.1 = (f32[80,128]{1,0:T(8,128)S(1)}, f32[8,128]{1,0:T(8,128)S(1)}) custom-call(f32[128,256]{1,0:T(8,128)S(1)} %copy-done.10, f32[128,128]{1,0:T(8,128)S(1)} %copy-done.11, f32[128,256]{1,0:T(8,128)S(1)} %get-tuple-element.33.self_grad, f32[128,256]{1,0:T(8,128)S(1)} %get-tuple-element.34.neigh_grad, f32[64,128]{1,0:T(8,128)S(1)} %get-tuple-element.35.head_grad, ...), custom_call_target="tpu_custom_call" | custom-call | tf_op jit(solution)/shard_map/reduce/pallas_call | solution.py:771
  104.9 0.7 fusion.2
  105.7 0.7 bitcast_compare_fusion
  106.4 0.1 copy.31
  106.5 0.1 copy.32
  106.6 0.1 copy.34
  106.7 0.4 fusion.3
  107.2 0.7 copy.35
  107.9 0.7 copy.36
  108.6 0.7 copy.37
  109.3 0.7 copy.38
  110.1 0.5 slice.6
  (33 shorter events, 0.5 us)
Async XLA Ops:
  4.8 1.2 %copy-start.8 = (bf16[2048,256]{1,0:T(8,128)(2,1)S(1)}, bf16[2048,256]{1,0:T(8,128)(2,1)}, u32[]{:S(2)}) copy-start(bf16[2048,256]{1,0:T(8,128)(2,1)} %feat.1) | copy-start | bytes 3145732
  6.0 0.7 copy-start.13
  6.7 0.7 copy-start.14
  40.2 2.0 %copy-start = (bf16[32,256,256]{2,1,0:T(8,128)(2,1)}, bf16[32,256,256]{2,1,0:T(8,128)(2,1)S(1)}, u32[]{:S(2)}) copy-start(bf16[32,256,256]{2,1,0:T(8,128)(2,1)S(1)} %get-tuple-element.24.enc) | copy-start | bytes 12582916
  42.2 1.9 %copy-start.3 = (bf16[4,2048,256]{2,1,0:T(8,128)(2,1)}, bf16[4,2048,256]{2,1,0:T(8,128)(2,1)S(1)}, u32[]{:S(2)}) copy-start(bf16[4,2048,256]{2,1,0:T(8,128)(2,1)S(1)} %get-tuple-element.30.fbuf) | copy-start | bytes 12582916
  44.1 0.6 copy-start.12
  44.7 17.6 %copy-start.6 = (bf16[848,256]{1,0:T(8,128)(2,1)}, bf16[848,256]{1,0:T(8,128)(2,1)S(1)}, u32[]{:S(2)}) copy-start(bf16[848,256]{1,0:T(8,128)(2,1)S(1)} %get-tuple-element.25.table) | copy-start | bytes 1302532
  44.7 17.6 %copy-start.7 = (bf16[3,256,256]{2,1,0:T(8,128)(2,1)}, bf16[3,256,256]{2,1,0:T(8,128)(2,1)S(1)}, u32[]{:S(2)}) copy-start(bf16[3,256,256]{2,1,0:T(8,128)(2,1)S(1)} %get-tuple-element.26.wtrans) | copy-start | bytes 1179652
  44.7 17.6 %copy-start.1 = (bf16[32,256,256]{2,1,0:T(8,128)(2,1)S(1)}, bf16[32,256,256]{2,1,0:T(8,128)(2,1)}, u32[]{:S(2)}) copy-start(bf16[32,256,256]{2,1,0:T(8,128)(2,1)} %copy-done) | copy-start | bytes 12582916
  44.7 17.6 %copy-start.9 = (s32[8192]{0:T(1024)S(1)}, s32[8192]{0:T(1024)}, u32[]{:S(2)}) copy-start(s32[8192]{0:T(1024)} %param.15) | copy-start | bytes 98308
  62.4 1.6 %copy-start.2 = (bf16[16,256,256]{2,1,0:T(8,128)(2,1)S(1)}, bf16[16,256,256]{2,1,0:T(8,128)(2,1)}, u32[]{:S(2)}) copy-start(bf16[16,256,256]{2,1,0:T(8,128)(2,1)} %forward.1.mean) | copy-start | bytes 6291460
  74.1 1.3 %copy-start.4 = (bf16[32,128,256]{2,1,0:T(8,128)(2,1)}, bf16[32,128,256]{2,1,0:T(8,128)(2,1)S(1)}, u32[]{:S(2)}) copy-start(bf16[32,128,256]{2,1,0:T(8,128)(2,1)S(1)} %get-tuple-element.28.sums) | copy-start | bytes 6291460
  75.4 1.4 %copy-start.5 = (f32[16,128,256]{2,1,0:T(8,128)}, f32[16,128,256]{2,1,0:T(8,128)S(1)}, u32[]{:S(2)}) copy-start(f32[16,128,256]{2,1,0:T(8,128)S(1)} %get-tuple-element.29.self_back) | copy-start | bytes 6291460
  76.8 29.6 %copy-start.16 = (f32[79,2,64]{0,2,1:T(8,128)S(1)}, f32[79,2,64]{0,2,1:T(8,128)}, u32[]{:S(2)}) copy-start(f32[79,2,64]{0,2,1:T(8,128)} %param.20) | copy-start | bytes 121348
  76.8 29.7 %copy-start.17 = (f32[79,2,64]{0,2,1:T(8,128)S(1)}, f32[79,2,64]{0,2,1:T(8,128)}, u32[]{:S(2)}) copy-start(f32[79,2,64]{0,2,1:T(8,128)} %param.21) | copy-start | bytes 121348
  76.8 29.8 %copy-start.15 = (f32[79,2,64]{0,2,1:T(8,128)S(1)}, f32[79,2,64]{0,2,1:T(8,128)}, u32[]{:S(2)}) copy-start(f32[79,2,64]{0,2,1:T(8,128)} %param.19) | copy-start | bytes 121348
  93.6 0.9 copy-start.10
  94.5 0.8 copy-start.11

commit v2 on v1

--- a/solution.py
+++ b/solution.py
@@ -28,7 +28,7 @@
 MESH = pl.DeviceIdType.MESH
 VM = pl.BlockSpec(memory_space=pltpu.VMEM)
 SM = pl.BlockSpec(memory_space=pltpu.SMEM)
-ANY = pl.BlockSpec(memory_space=pl.ANY)
+HBM = pl.BlockSpec(memory_space=pltpu.HBM)
 
 
 def sds(shape, dtype):
@@ -66,14 +66,21 @@
     return jax.nn.sigmoid(v)
 
 
+def remote(src, dst, send, recv, dev):
+    return pltpu.make_async_remote_copy(
+        src_ref=src, dst_ref=dst, send_sem=send, recv_sem=recv, device_id=dev, device_id_type=MESH
+    )
+
+
 def gather_kernel(
     ng,
     feat,
-    wmsg,
-    srow,
+    master,
+    pieces,
     labels,
     mask,
     pairs,
+    degree,
     tcount,
     fbuf,
     enc,
@@ -81,12 +88,20 @@
     wtrans,
     hot,
     marks,
+    inverse,
     lists,
+    mbuf,
+    pcs,
+    lab,
+    msk,
+    prs,
+    deg,
+    lbuf,
+    wmsg,
     pmsg,
     wbuf,
-    prow,
     local_sem,
-    core_sem,
+    small_sem,
     mark_sem,
     ws_core,
     ws_x,
@@ -96,36 +111,58 @@
     wr_recv,
     xs_send,
     xs_recv,
-    rl_send,
-    rl_recv,
+    en_send,
+    en_recv,
 ):
     g, q, k, x, partner, across = place()
     rows = feat.shape[0]
-    chunks = rows // B
-    blocks = chunks
+    blocks = rows // B
     sp = wmsg.shape[1]
-    tiles = pairs.shape[1]
+    slots = pieces.shape[1]
+    count = pairs.shape[2]
     tpad = lists.shape[1]
-
-    load = pltpu.make_async_copy(feat, fbuf.at[q], local_sem)
+    width = master.shape[1]
+
+    load = pltpu.make_async_copy(feat, fbuf.at[x], local_sem)
     load.start()
-    marks[x] = jnp.where(mask[...] > 0, labels[...], -1)
+    small = [
+        pltpu.make_async_copy(a, b, small_sem.at[i])
+        for i, (a, b) in enumerate(
+            [
+                (master, mbuf),
+                (pieces, pcs),
+                (labels, lab),
+                (mask, msk),
+                (pairs, prs),
+                (degree.at[k], deg.at[0]),
+                (degree.at[2 + k], deg.at[1]),
+            ]
+        )
+    ]
+    for copy in small:
+        copy.start()
 
     barrier = pltpu.get_barrier_semaphore()
+    pl.semaphore_signal(barrier, inc=1, device_id=(g, across), device_id_type=MESH)
     pl.semaphore_signal(barrier, inc=1, device_id=(g, partner), device_id_type=MESH)
-    pl.semaphore_signal(barrier, inc=1, device_id=(g, across), device_id_type=MESH)
 
     def greet(d, c):
         pl.semaphore_signal(barrier, inc=1, device_id=((g + d) % ng, q), device_id_type=MESH)
         return c
 
     lax.fori_loop(1, ng, greet, 0)
+
+    for copy in small:
+        copy.wait()
+    for j in range(PR):
+        cols = jnp.concatenate(
+            [mbuf[j], jnp.zeros((width, HALF - slots), f32)], axis=1
+        )
+        turned = jnp.transpose(jnp.concatenate([cols, jnp.zeros_like(cols)], axis=0))
+        other = pltpu.roll(turned, width, 1)
+        wmsg[j] = jnp.where(k == 0, turned, other)[:sp].astype(bf16)
+    marks[x] = jnp.where(msk[...] > 0, lab[...], -1)
     pl.semaphore_wait(barrier, ng + 1)
-
-    def remote(src, dst, send, recv, dev):
-        return pltpu.make_async_remote_copy(
-            src_ref=src, dst_ref=dst, send_sem=send, recv_sem=recv, device_id=dev, device_id_type=MESH
-        )
 
     first = remote(wmsg, pmsg, ws_core.at[0], ws_core.at[1], (g, partner))
     first.start()
@@ -134,13 +171,10 @@
     load.wait()
 
     def cross(i):
-        piece = fbuf.at[q, pl.ds(pl.multiple_of(i * B, B), B)]
+        piece = fbuf.at[x, pl.ds(pl.multiple_of(i * B, B), B)]
         return remote(piece, piece, xs_send.at[i], xs_recv.at[i], (g, across))
 
     cross(0).start()
-    share = remote(fbuf.at[q], fbuf.at[q], core_sem.at[0], core_sem.at[1], (g, partner))
-    share.start()
-
     first.wait()
     wbuf[k, g, x] = wmsg[k] + pmsg[k]
     second = remote(wbuf.at[k, g, x], wbuf.at[k, g, x], ws_x.at[0], ws_x.at[1], (g, across))
@@ -150,7 +184,7 @@
         cross(i).start()
         return c
 
-    lax.fori_loop(1, chunks, cross_all, 0)
+    lax.fori_loop(1, blocks, cross_all, 0)
     second.wait()
 
     def to_group(d):
@@ -182,13 +216,10 @@
     hand_over(0).start()
 
     shift = blocks.bit_length() - 1
-    prow[...] = jnp.zeros_like(prow)
-    pick = (
-        lax.broadcasted_iota(jnp.int32, (8, 2), 0) == lax.broadcasted_iota(jnp.int32, (8, 2), 1)
-    ).astype(bf16)
-    prow[:, :tiles] = dot_nt(pick, pairs[0].astype(f32).astype(bf16))
-    rvec = prow[0:1, :].astype(jnp.int32)
-    cvec = prow[1:2, :].astype(jnp.int32)
+    fill = jnp.zeros((2, tpad - count), jnp.int32)
+    both = jnp.concatenate([prs[0], fill], axis=1)
+    rvec = both[0:1]
+    cvec = both[1:2]
     tvec = lax.broadcasted_iota(jnp.int32, (1, tpad), 1)
     live = tvec < tcount[0]
 
@@ -221,11 +252,26 @@
 
     ft, fr, fc, fn = compact(fmine, frow, cvec)
     bt, bc, br, bn = compact(bmine, bcol, rvec)
-    lists[...] = jnp.concatenate([ft, fr, fc, bt, bc, br, fn, bn], axis=0)
-
-    hot[...] = (
-        (lax.broadcasted_iota(jnp.int32, hot.shape, 0) == srow[...]).astype(f32).astype(bf16)
-    )
+    lbuf[...] = jnp.concatenate([ft, fr, fc, bt, bc, br, fn, bn], axis=0)
+    put = pltpu.make_async_copy(lbuf, lists, local_sem)
+    put.start()
+    inverse[...] = 1.0 / deg[...].astype(f32)
+
+    lanes = ng * sp
+    piece = jnp.concatenate([pcs[...], jnp.full((ng, HALF - slots), -1, jnp.int32)], axis=1)
+    high = lax.shift_right_logical(piece + 1, 4).astype(f32).astype(bf16)
+    low = ((piece + 1) & 15).astype(f32).astype(bf16)
+    lane = lax.broadcasted_iota(jnp.int32, (1, lanes), 1)
+    owner = jnp.floor((lane.astype(f32) + 0.5) * (1.0 / sp)).astype(jnp.int32)
+    within = lane - owner * sp
+    pick = (lax.broadcasted_iota(jnp.int32, (HALF, lanes), 0) == within).astype(f32).astype(bf16)
+    wide = dot_nn(high, pick) * 16.0 + dot_nn(low, pick)
+    keep = lax.broadcasted_iota(jnp.int32, (ng, lanes), 0) == owner
+    flat = jnp.sum(jnp.where(keep, wide, 0.0), axis=0, keepdims=True).astype(jnp.int32) - 1
+    line = lax.broadcasted_iota(jnp.int32, (TROWS, lanes), 0)
+    for j in range(PR):
+        at = jnp.where(flat >= 0, flat * PR + j, -1)
+        hot[:, j * lanes : (j + 1) * lanes] = (line == at).astype(f32).astype(bf16)
 
     def pass_on(d, c):
         from_group(d).wait_recv()
@@ -247,65 +293,52 @@
     for i in range(3):
         wtrans[i] = jnp.transpose(full[i * B : (i + 1) * B]).astype(bf16)
     bias = column_of(table[PROWS - 2 : PROWS + 14], 0)
-    bias = jnp.concatenate([bias, bias], axis=1)
-
-    def encode(quarter, i):
-        piece = fbuf[quarter, pl.ds(pl.multiple_of(i * B, B), B)]
+    bias = jnp.concatenate([bias] * 4, axis=1)
+
+    def share(i, core):
+        away = i // (blocks // 2)
+        quarter = (x + away * (1 - 2 * x)) * 2 + core
+        piece = enc.at[pl.ds(quarter * blocks + (i % (blocks // 2)) * 2, 2)]
+        return remote(piece, piece, en_send.at[i], en_recv.at[i], (g, partner))
+
+    def encode(i):
+        away = i // (blocks // 2)
+        side = x + away * (1 - 2 * x)
+        base = (i % (blocks // 2)) * 2
+        piece = fbuf[side, pl.ds(pl.multiple_of(base * B, 2 * B), 2 * B)]
         pre = dot_nt(wtrans[0], piece) + bias
-        enc[quarter * blocks + i] = (pre * sigmoid(pre)).astype(bf16)
+        out = (pre * sigmoid(pre)).astype(bf16)
+        at = (side * 2 + k) * blocks + base
+        enc[at] = out[:, :B]
+        enc[at + 1] = out[:, B:]
+        share(i, k).start()
 
     def own(i, c):
-        encode(q, i)
-        return c
-
-    lax.fori_loop(0, blocks, own, 0)
-    share.wait_recv()
-
-    def near(i, c):
-        encode(partner, i)
-        return c
-
-    lax.fori_loop(0, blocks, near, 0)
-    mine_far = across
-    near_far = partner + 2 - 4 * x
+        encode(i)
+        return c
+
+    lax.fori_loop(0, blocks // 2, own, 0)
 
     def crossed(i):
-        piece = fbuf.at[mine_far, pl.ds(pl.multiple_of(i * B, B), B)]
+        piece = fbuf.at[1 - x, pl.ds(pl.multiple_of(i * B, B), B)]
         return remote(piece, piece, xs_send.at[i], xs_recv.at[i], (g, across))
 
-    def relay(i):
-        piece = fbuf.at[mine_far, pl.ds(pl.multiple_of(i * B, B), B)]
-        return remote(piece, piece, rl_send.at[i], rl_recv.at[i], (g, partner))
-
-    def relayed(i):
-        piece = fbuf.at[near_far, pl.ds(pl.multiple_of(i * B, B), B)]
-        return remote(piece, piece, rl_send.at[i], rl_recv.at[i], (g, partner))
-
     def far(i, c):
-        crossed(i).wait_recv()
-        relay(i).start()
-        encode(mine_far, i)
-
-        @pl.when(i > 0)
-        def _():
-            relayed(i - 1).wait_recv()
-            encode(near_far, i - 1)
-
-        return c
-
-    lax.fori_loop(0, chunks, far, 0)
-    relayed(chunks - 1).wait_recv()
-    encode(near_far, chunks - 1)
-
+        crossed(2 * i).wait_recv()
+        crossed(2 * i + 1).wait_recv()
+        encode(blocks // 2 + i)
+        return c
+
+    lax.fori_loop(0, blocks // 2, far, 0)
+
+    def settle(i, c):
+        share(i, 1 - k).wait_recv()
+        share(i, k).wait_send()
+        cross(i).wait_send()
+        return c
+
+    lax.fori_loop(0, blocks, settle, 0)
     mark_copy.wait()
-    share.wait_send()
-
-    def drain(i, c):
-        cross(i).wait_send()
-        relay(i).wait_send()
-        return c
-
-    lax.fori_loop(0, chunks, drain, 0)
 
     def drain_group(d, c):
         to_group(d).wait_send()
@@ -314,31 +347,63 @@
 
     lax.fori_loop(1, ng, drain_group, 0)
     hand_over(0).wait_send()
-
-
-def forward_kernel(lists, tiles, enc, degree, mean, acc):
-    k = lax.axis_index("col") % 2
-    local = mean.shape[0]
-    blocks = local // 2
-
-    def clear(i, c):
-        acc[i] = jnp.zeros((B, B), f32)
-        return c
-
-    lax.fori_loop(0, local + 1, clear, 0)
-    count = lists[6, 0]
+    put.wait()
+
+
+RING = 32
+
+
+def each_tile(tiles, order, count, ring, sems, use):
+    def fetch(j):
+        return pltpu.make_async_copy(tiles.at[order(j)], ring.at[j % RING], sems.at[j % RING])
+
+    def ask(j):
+        @pl.when(j < count)
+        def _():
+            fetch(j).start()
+
+    def first(j, c):
+        ask(j)
+        return c
+
+    lax.fori_loop(0, RING, first, 0)
 
     def step(i, c):
         for u in range(UNROLL):
             j = i * UNROLL + u
-            r = lists[1, j]
-            acc[r] += dot_nt(enc[lists[2, j]], tiles[lists[0, j]])
-        return c
-
-    lax.fori_loop(0, (count + UNROLL - 1) // UNROLL, step, 0)
+
+            @pl.when(j < count)
+            def _():
+                fetch(j).wait()
+
+        for u in range(UNROLL):
+            j = i * UNROLL + u
+            use(j, ring[j % RING])
+        for u in range(UNROLL):
+            ask(i * UNROLL + u + RING)
+        return c
+
+    return lambda: lax.fori_loop(0, (count + UNROLL - 1) // UNROLL, step, 0)
+
+
+def forward_kernel(lists, tiles, enc, inverse, mean, acc, ring, sems):
+    local = mean.shape[0]
+    blocks = local // 2
+
+    def use(j, tile):
+        acc[lists[1, j]] += dot_nt(enc[lists[2, j]], tile)
+
+    run = each_tile(tiles, lambda j: lists[0, j], lists[6, 0], ring, sems, use)
+
+    def clear(i, c):
+        acc[i] = jnp.zeros((B, B), f32)
+        return c
+
+    lax.fori_loop(0, local + 1, clear, 0)
+    run()
 
     def finish(i, c):
-        scale = 1.0 / degree[(i // blocks) * 2 + k, :, pl.ds(pl.multiple_of((i % blocks) * B, B), B)].astype(f32)
+        scale = inverse[i // blocks, :, pl.ds(pl.multiple_of((i % blocks) * B, B), B)]
         mean[i] = (acc[i] * scale).astype(bf16)
         return c
 
@@ -351,7 +416,7 @@
     table,
     wtrans,
     marks,
-    degree,
+    inverse,
     sums,
     self_back,
     self_grad,
@@ -417,7 +482,7 @@
         grad = ((expd * (1.0 / total) - onehot) * valid).astype(bf16)
         back = dot_tn(head, grad) * (sig * (1.0 + pre * (1.0 - sig)))
         sgrad = back.astype(bf16)
-        scale = 1.0 / degree[(i // (steps // 2)) * 2 + k, :, cols].astype(f32)
+        scale = inverse[i // (steps // 2), :, cols]
         out = (dot_nn(neigh_half, sgrad) * scale).astype(bf16)
         for b in range(2):
             lanes = slice(b * B, (b + 1) * B)
@@ -457,35 +522,29 @@
     lax.fori_loop(0, steps, done, 0)
 
 
-def backward_kernel(lists, tiles, sums, self_back, fbuf, table, wtrans, enc_grad, bias_grad, acc):
-    q = lax.axis_index("col")
-    k = q % 2
-    x = q // 2
+def backward_kernel(lists, tiles, sums, self_back, fbuf, table, wtrans, enc_grad, bias_grad, acc, ring, sems):
+    x = lax.axis_index("col") // 2
     local = self_back.shape[0]
     blocks = local // 2
 
+    def use(j, tile):
+        acc[lists[4, j]] += dot_nn(sums[lists[5, j]], tile)
+
+    run = each_tile(tiles, lambda j: lists[3, j], lists[7, 0], ring, sems, use)
+
     def clear(i, c):
         acc[i] = jnp.zeros((HALF, B), f32)
         return c
 
     lax.fori_loop(0, local + 1, clear, 0)
-    count = lists[7, 0]
-
-    def step(i, c):
-        for u in range(UNROLL):
-            j = i * UNROLL + u
-            acc[lists[4, j]] += dot_nn(sums[lists[5, j]], tiles[lists[3, j]])
-        return c
-
-    lax.fori_loop(0, (count + UNROLL - 1) // UNROLL, step, 0)
-
+    run()
     half = pl.ds(pl.multiple_of(x * HALF, HALF), HALF)
     wide = column_of(table[PROWS - 2 : PROWS + 14, half], 0)
     wide = jnp.concatenate([wide, wide], axis=1)
     weight = wtrans[0, half]
     eg = bg = None
     for b in range(local):
-        piece = fbuf[(b // blocks) * 2 + k, (b % blocks) * B : (b % blocks + 1) * B]
+        piece = fbuf[b // blocks, (b % blocks) * B : (b % blocks + 1) * B]
         pre = dot_nt(weight, piece) + wide
         sig = sigmoid(pre)
         grad = ((self_back[b] + acc[b]) * (sig * (1.0 + pre * (1.0 - sig)))).astype(bf16)
@@ -561,11 +620,6 @@
     pbuf[1] = spread(rolled, whole)
     pl.semaphore_wait(barrier, ng)
 
-    def remote(src, dst, send, recv, dev):
-        return pltpu.make_async_remote_copy(
-            src_ref=src, dst_ref=dst, send_sem=send, recv_sem=recv, device_id=dev, device_id_type=MESH
-        )
-
     one = remote(pbuf.at[1 - k], rbuf, core_sem.at[0], core_sem.at[1], (g, partner))
     one.start()
     two = remote(sbuf, srecv, stat_sem.at[0], stat_sem.at[1], (g, partner))
@@ -628,6 +682,38 @@
         return c
 
     lax.fori_loop(1, ng, finish, 0)
+
+
+def update_kernel(packed, loss, pieces, master, first, second, new_master, new_first, new_second, low, mean_loss):
+    g = lax.axis_index("grp")
+    slots = pieces.shape[1]
+    width = master.shape[1]
+    sp = packed.shape[0]
+    rows = packed[...]
+    if sp < HALF:
+        rows = jnp.concatenate([rows, jnp.zeros((HALF - sp, HALF), f32)], axis=0)
+    turned = jnp.transpose(rows)
+    piece = pieces[pl.ds(g, 1), :]
+    owned = piece >= 0
+    for j in range(PR):
+        grad = turned[j * width : (j + 1) * width, :slots]
+        decay = jnp.where(piece * PR + j < PROWS - 2, decay_rate, 0.0)
+        old = master[j]
+        one = beta_one * first[j] + (1.0 - beta_one) * grad
+        two = beta_two * second[j] + (1.0 - beta_two) * grad * grad
+        one_hat = one / (1.0 - beta_one**STEP)
+        two_hat = two / (1.0 - beta_two**STEP)
+        new = old - learn_rate * (one_hat / (jnp.sqrt(two_hat) + adam_epsilon) + decay * old)
+        new = jnp.where(owned, new, 0.0)
+        new_master[j] = new
+        new_first[j] = jnp.where(owned, one, 0.0)
+        new_second[j] = jnp.where(owned, two, 0.0)
+        low[j] = new.astype(bf16)
+    mean_loss[0, 0] = loss[0, 0]
+
+
+def far(v):
+    return pltpu.with_memory_space_constraint(v, pltpu.HBM)
 
 
 def params(limit, collective=None):
@@ -654,52 +740,46 @@
 ):
     nc = lax.axis_size("col")
     ng = lax.axis_size("grp")
-    q = lax.axis_index("col")
-    grp_index = lax.axis_index("grp")
     rows = features.shape[0]
     blocks = rows // B
     nb = nc * blocks
     local = 2 * blocks
-    tile_slots = adj_tiles.shape[0]
-    tpad = -(-tile_slots // HALF) * HALF
+    count = adj_tiles.shape[0]
+    tpad = -(-count // HALF) * HALF
     slots = slot_piece.shape[1]
     sp = -(-slots // 16) * 16
     width = master.shape[2]
-    chunks = blocks
-
-    flat = jnp.transpose(master.astype(bf16), (1, 0, 2))
-    flat = jnp.pad(flat, ((0, 0), (0, sp - slots), (0, 0)))
-    empty = jnp.zeros_like(flat)
-    wmsg = jnp.where(
-        q % 2 == 0,
-        jnp.concatenate([flat, empty], axis=2),
-        jnp.concatenate([empty, flat], axis=2),
-    )
-    piece = jnp.pad(slot_piece, ((0, 0), (0, sp - slots)), constant_values=-1).reshape(1, -1)
-    srow = jnp.concatenate(
-        [jnp.where(piece >= 0, piece * PR + j, -1) for j in range(PR)], axis=1
-    )
-    degree_rows = degree.reshape(nc, 1, rows)
-
-    fbuf, enc, table, wtrans, hot, marks, lists = pl.pallas_call(
+    master_t = jnp.transpose(master, (1, 2, 0))
+    first_t = jnp.transpose(moment_one, (1, 2, 0))
+    second_t = jnp.transpose(moment_two, (1, 2, 0))
+
+    fbuf, enc, table, wtrans, hot, marks, inverse, lists = pl.pallas_call(
         functools.partial(gather_kernel, ng),
         out_shape=(
-            sds((nc, rows, F), bf16),
-            sds((nb, HID, B), bf16),
-            sds((TROWS, HID), bf16),
-            sds((3, HID, HID), bf16),
-            sds((TROWS, 2 * ng * sp), bf16),
-            sds((2, 1, rows), jnp.int32),
+            pltpu.VMEM((2, rows, F), bf16),
+            pltpu.VMEM((nb, HID, B), bf16),
+            pltpu.VMEM((TROWS, HID), bf16),
+            pltpu.VMEM((3, HID, HID), bf16),
+            pltpu.VMEM((TROWS, 2 * ng * sp), bf16),
+            pltpu.VMEM((2, 1, rows), jnp.int32),
+            pltpu.VMEM((2, 1, rows), f32),
             sds((8, tpad), jnp.int32),
         ),
-        in_specs=[ANY, VM, VM, VM, VM, VM, SM],
-        out_specs=(VM,) * 7,
+        in_specs=[HBM] * 7 + [SM],
+        out_specs=(VM,) * 7 + (HBM,),
         scratch_shapes=[
+            pltpu.VMEM((PR, width, slots), f32),
+            pltpu.VMEM((ng, slots), jnp.int32),
+            pltpu.VMEM((1, rows), jnp.int32),
+            pltpu.VMEM((1, rows), jnp.int32),
+            pltpu.VMEM((1, 2, count), jnp.int32),
+            pltpu.VMEM((2, 1, rows), jnp.int32),
+            pltpu.VMEM((8, tpad), jnp.int32),
+            pltpu.VMEM((2, sp, HALF), bf16),
             pltpu.VMEM((2, sp, HALF), bf16),
             pltpu.VMEM((2, ng, 2, sp, HALF), bf16),
-            pltpu.VMEM((8, tpad), f32),
             DMA,
-            DMA((2,)),
+            DMA((7,)),
             DMA((2,)),
             DMA((2,)),
             DMA((2,)),
@@ -707,43 +787,45 @@
             DMA((ng,)),
             DMA((ng,)),
             DMA((ng,)),
-            DMA((chunks,)),
-            DMA((chunks,)),
-            DMA((chunks,)),
-            DMA((chunks,)),
+            DMA((blocks,)),
+            DMA((blocks,)),
+            DMA((blocks,)),
+            DMA((blocks,)),
         ],
-        compiler_params=params(24, 0),
+        compiler_params=params(12, 0),
         name="gather",
     )(
-        features,
-        wmsg,
-        srow,
-        labels.reshape(1, rows),
-        loss_mask.reshape(1, rows),
-        block_pairs,
+        far(features),
+        far(master_t),
+        far(slot_piece),
+        far(labels.reshape(1, rows)),
+        far(loss_mask.reshape(1, rows)),
+        far(jnp.transpose(block_pairs, (0, 2, 1))),
+        far(degree.reshape(nc, 1, rows)),
         tile_count,
     )
 
+    adj = far(adj_tiles)
     mean = pl.pallas_call(
         forward_kernel,
-        out_shape=sds((local, HID, B), bf16),
-        in_specs=[SM, VM, VM, VM],
+        out_shape=pltpu.VMEM((local, HID, B), bf16),
+        in_specs=[SM, HBM, VM, VM],
         out_specs=VM,
-        scratch_shapes=[pltpu.VMEM((local + 1, HID, B), f32)],
-        compiler_params=params(56),
+        scratch_shapes=[pltpu.VMEM((local + 1, HID, B), f32), pltpu.VMEM((RING, B, B), bf16), DMA((RING,))],
+        compiler_params=params(14),
         name="forward",
-    )(lists, adj_tiles, enc, degree_rows)
+    )(lists, adj, enc, inverse)
 
     sums, self_back, self_grad, neigh_grad, head_grad, bsage, stats = pl.pallas_call(
         sage_kernel,
         out_shape=(
-            sds((nb, HALF, B), bf16),
-            sds((local, HALF, B), f32),
-            sds((HALF, HID), f32),
-            sds((HALF, HID), f32),
-            sds((CLS, HALF), f32),
-            sds((HALF, HALF), f32),
-            sds((8, 2 * B), f32),
+            pltpu.VMEM((nb, HALF, B), bf16),
+            pltpu.VMEM((local, HALF, B), f32),
+            pltpu.VMEM((HALF, HID), f32),
+            pltpu.VMEM((HALF, HID), f32),
+            pltpu.VMEM((CLS, HALF), f32),
+            pltpu.VMEM((HALF, HALF), f32),
+            pltpu.VMEM((8, 2 * B), f32),
         ),
         in_specs=[VM] * 6,
         out_specs=(VM,) * 7,
@@ -754,23 +836,23 @@
             DMA((blocks,)),
             DMA((blocks,)),
         ],
-        compiler_params=params(24, 1),
+        compiler_params=params(12, 1),
         name="sage",
-    )(enc, mean, table, wtrans, marks, degree_rows)
+    )(enc, mean, table, wtrans, marks, inverse)
 
     enc_grad, benc = pl.pallas_call(
         backward_kernel,
-        out_shape=(sds((HALF, F), f32), sds((HALF, HALF), f32)),
-        in_specs=[SM, VM, VM, VM, VM, VM, VM],
+        out_shape=(pltpu.VMEM((HALF, F), f32), pltpu.VMEM((HALF, HALF), f32)),
+        in_specs=[SM, HBM, VM, VM, VM, VM, VM],
         out_specs=(VM,) * 2,
-        scratch_shapes=[pltpu.VMEM((local + 1, HALF, B), f32)],
-        compiler_params=params(56),
+        scratch_shapes=[pltpu.VMEM((local + 1, HALF, B), f32), pltpu.VMEM((RING, B, B), bf16), DMA((RING,))],
+        compiler_params=params(12),
         name="backward",
-    )(lists, adj_tiles, sums, self_back, fbuf, table, wtrans)
+    )(lists, adj, sums, self_back, fbuf, table, wtrans)
 
     packed, loss = pl.pallas_call(
         functools.partial(reduce_kernel, ng),
-        out_shape=(sds((sp, HALF), f32), sds((8, HALF), f32)),
+        out_shape=(pltpu.VMEM((sp, HALF), f32), pltpu.VMEM((8, HALF), f32)),
         in_specs=[VM] * 8,
         out_specs=(VM,) * 2,
         scratch_shapes=[
@@ -789,29 +871,24 @@
             DMA((ng,)),
             DMA((ng,)),
         ],
-        compiler_params=params(24, 2),
+        compiler_params=params(12, 2),
         name="reduce",
     )(enc_grad, benc, self_grad, neigh_grad, head_grad, bsage, hot, stats)
 
-    mean_loss = loss[0, 0]
-    my_pieces = lax.dynamic_slice_in_dim(slot_piece, grp_index, 1, 0)[0]
-    is_owned = my_pieces >= 0
-    safe_pieces = jnp.where(is_owned, my_pieces, 0)
-    owned_values = is_owned[:, None, None]
-    slot_grad = jnp.where(owned_values, packed[:slots].reshape(slots, PR, width), 0.0)
-    table_rows = safe_pieces[:, None] * PR + jnp.arange(PR, dtype=jnp.int32)[None, :]
-    decay_values = jnp.where(table_rows < PROWS - 2, decay_rate, 0.0)[:, :, None]
-    first_moment = beta_one * moment_one + (1.0 - beta_one) * slot_grad
-    second_moment = beta_two * moment_two + (1.0 - beta_two) * slot_grad * slot_grad
-    first_hat = first_moment / (1.0 - beta_one**STEP)
-    second_hat = second_moment / (1.0 - beta_two**STEP)
-    updated = master - learn_rate * (
-        first_hat / (jnp.sqrt(second_hat) + adam_epsilon) + decay_values * master
-    )
-    updated = jnp.where(owned_values, updated, 0.0)
-    first_moment = jnp.where(owned_values, first_moment, 0.0)
-    second_moment = jnp.where(owned_values, second_moment, 0.0)
-    return (mean_loss, updated, first_moment, second_moment, updated.astype(jnp.bfloat16))
+    shape = (PR, width, slots)
+    new_master, new_first, new_second, low, mean_loss = pl.pallas_call(
+        update_kernel,
+        out_shape=(sds(shape, f32), sds(shape, f32), sds(shape, f32), sds(shape, bf16), sds((1, 1), f32)),
+        in_specs=[VM] * 6,
+        out_specs=(VM,) * 4 + (SM,),
+        compiler_params=params(4),
+        name="update",
+    )(packed, loss, slot_piece, master_t, first_t, second_t)
+
+    def back(v):
+        return jnp.transpose(v, (2, 0, 1))
+
+    return mean_loss[0, 0], back(new_master), back(new_first), back(new_second), back(low)
 
 
 def solution(mesh):

time: 111 us -> 72.7 us (0.65)
  local copies, waits for them, and re-layouts: 18.1 us -> 0.03 us
  Pallas kernels: 86.7 us -> 70.5 us
  other arithmetic: 4.26 us -> 0 us
    unnamed x44 -> x8, local copies, waits for them, and re-layouts: 17.2 us -> 0.03 us
    pallas_call x5 -> x6, Pallas kernels: 86.7 us -> 70.5 us  [the longest x1 33.2 us: body(): pl.pallas_call(functools.partial(gather_kernel, ng), out_shape=(pltpu.VME...]
    ge x2 -> x0, other arithmetic: 1.4 us -> none  [the longest x1 0.7 us: body(): is_owned = my_pieces >= 0]
    mul x2 -> x0, other arithmetic: 1.39 us -> none  [the longest x1 0.7 us: body(): safe_pieces[:, None] * PR + jnp.arange(PR, dtype=jnp.int32)[None, :]]
    convert_element_type x2 -> x0, other arithmetic: 1.3 us -> none  [the longest x1 0.85 us: body(): flat = jnp.transpose(master.astype(bf16), (1, 0, 2))]
where the time goes in v2:
time: 72.7 us; the launch traced here: 71.9 us
  Pallas kernels  70.5 us (97%)
  between operations  1.38 us (2%)
    pallas_call x1, Pallas kernels, body(): pl.pallas_call(functools.partial(gather_kernel, ng), out_shape=(pltpu.VME...  33.2 us
    pallas_call x1, Pallas kernels, body(): pl.pallas_call(sage_kernel, out_shape=(pltpu.VMEM((nb, HALF, B), bf16), p...  9.96 us
    pallas_call x1, Pallas kernels, body(): pl.pallas_call(functools.partial(reduce_kernel, ng), out_shape=(pltpu.VME...  9.45 us
    pallas_call x1, Pallas kernels, body(): pl.pallas_call(forward_kernel, out_shape=pltpu.VMEM((local, HID, B), bf16...  8.9 us
    pallas_call x1, Pallas kernels, body(): pl.pallas_call(backward_kernel, out_shape=(pltpu.VMEM((HALF, F), f32), pl...  8.19 us

profile of v2, /device:TPU:0, one launch (start us, length us, event | category | flops | bytes accessed | tf_op | source)
XLA Modules:
  0.0 71.9 jit_solution(11942574551539223434)
XLA Ops:
  1.3 33.2 %gather.1 = (bf16[2,2048,256]{2,1,0:T(8,128)(2,1)S(1)}, bf16[32,256,256]{2,1,0:T(8,128)(2,1)S(1)}, bf16[848,256]{1,0:T(8,128)(2,1)S(1)}, bf16[3,256,256]{2,1,0:T...) custom-call(bf16[2048,256]{1,0:T(8,128)(2,1)} %feat.1, ...), custom_call_target="tpu_custom_call" | custom-call | tf_op jit(solution)/shard_map/gather/pallas_call | solution.py:756
  34.5 8.9 %forward.1.mean = bf16[16,256,256]{2,1,0:T(8,128)(2,1)S(1)} custom-call(s32[8,256]{1,0:T(8,128)S(1)} %get-tuple-element.29.lists, bf16[192,256,256]{2,1,0:T(8,128)(2,1)} %tiles.3, bf16[32,256,256]{2,1,0:T(8,128)(2,1)S(1)} %get-tuple-element.30.enc, f32[2,1,2048]{2,1,0:T(1,128)S(1)} %get-tuple-element.31.inverse), custom_call_target="tpu_custom_call" | custom-call | tf_op jit(solution)/shard_map/forward/pallas_call | solution.py:809
  43.4 10.0 %sage.1 = (bf16[32,128,256]{2,1,0:T(8,128)(2,1)S(1)}, f32[16,128,256]{2,1,0:T(8,128)S(1)}, f32[128,256]{1,0:T(8,128)S(1)}, f32[128,256]{1,0:T(8,128)S(1)}, f32[6...) custom-call(bf16[32,256,256]{2,1,0:T(8,128)(2,1)S(1)} %get-tuple-element.30.enc, ...), custom_call_target="tpu_custom_call" | custom-call | tf_op jit(solution)/shard_map/sage/pallas_call | solution.py:819
  53.4 8.2 %backward.1 = (f32[128,256]{1,0:T(8,128)S(1)}, f32[128,128]{1,0:T(8,128)S(1)}) custom-call(s32[8,256]{1,0:T(8,128)S(1)} %get-tuple-element.29.lists, bf16[192,256,256]{2,1,0:T(8,128)(2,1)} %tiles.3, bf16[32,128,256]{2,1,0:T(8,128)(2,1)S(1)} %get-tuple-element.35.sums, f32[16,128,256]{2,1,0:T(8,128)S(1)} %get-tuple-element.36.self_back, ...), custom_call_target="tpu_custom_call" | custom-call | tf_op jit(solution)/shard_map/backward/pallas_call | solution.py:843
  61.6 0.0 copy-start
  61.6 0.0 copy-start.1
  61.6 0.0 copy-start.2
  61.6 0.0 copy-start.3
  61.6 9.4 %reduce.1 = (f32[80,128]{1,0:T(8,128)S(1)}, f32[8,128]{1,0:T(8,128)S(1)}) custom-call(f32[128,256]{1,0:T(8,128)S(1)} %get-tuple-element.38.enc_grad, f32[128,128]{1,0:T(8,128)S(1)} %get-tuple-element.39.benc_grad, f32[128,256]{1,0:T(8,128)S(1)} %get-tuple-element.40.self_grad, f32[128,256]{1,0:T(8,128)S(1)} %get-tuple-element.41.neigh_grad, ...), custom_call_target="tpu_custom_call" | custom-call | tf_op jit(solution)/shard_map/reduce/pallas_call | solution.py:853
  71.1 0.0 copy-done
  71.1 0.0 copy-done.1
  71.1 0.0 copy-done.2
  71.1 0.0 copy-done.3
  71.1 0.8 %update.1 = (f32[2,64,79]{2,1,0:T(8,128)}, f32[2,64,79]{2,1,0:T(8,128)}, f32[2,64,79]{2,1,0:T(8,128)}, bf16[2,64,79]{2,1,0:T(8,128)(2,1)}, f32[1,1]{1,0:T(1,128)}) custom-call(f32[80,128]{1,0:T(8,128)S(1)} %get-tuple-element.46.packed, f32[8,128]{1,0:T(8,128)S(1)} %get-tuple-element.47.loss, s32[8,79]{1,0:T(8,128)S(1)} %copy-done.3, ...), custom_call_target="tpu_custom_call" | custom-call | tf_op jit(solution)/shard_map/update/pallas_call | solution.py:879
Async XLA Ops:
  61.6 9.5 %copy-start = (f32[79,2,64]{0,2,1:T(8,128)S(1)}, f32[79,2,64]{0,2,1:T(8,128)}, u32[]{:S(2)}) copy-start(f32[79,2,64]{0,2,1:T(8,128)} %param.19) | copy-start | bytes 121348
  61.6 9.5 %copy-start.1 = (f32[79,2,64]{0,2,1:T(8,128)S(1)}, f32[79,2,64]{0,2,1:T(8,128)}, u32[]{:S(2)}) copy-start(f32[79,2,64]{0,2,1:T(8,128)} %param.20) | copy-start | bytes 121348
  61.6 9.5 %copy-start.2 = (f32[79,2,64]{0,2,1:T(8,128)S(1)}, f32[79,2,64]{0,2,1:T(8,128)}, u32[]{:S(2)}) copy-start(f32[79,2,64]{0,2,1:T(8,128)} %param.21) | copy-start | bytes 121348
  61.6 9.5 %copy-start.3 = (s32[8,79]{1,0:T(8,128)S(1)}, s32[8,79]{1,0:T(8,128)}, u32[]{:S(2)}) copy-start(s32[8,79]{1,0:T(8,128)} %pieces.3) | copy-start | bytes 7588

commit v3 on v2

--- a/solution.py
+++ b/solution.py
@@ -72,6 +72,49 @@
     )
 
 
+def enter(ng, g, q, others):
+    barrier = pltpu.get_barrier_semaphore()
+    line, last = g // 2, ng // 2 - 1
+    for c in others:
+        pl.semaphore_signal(barrier, inc=1, device_id=(g, c), device_id_type=MESH)
+    pair = g + 1 - 2 * (g % 2)
+    pl.semaphore_signal(barrier, inc=1, device_id=(pair, q), device_id_type=MESH)
+
+    @pl.when(line > 0)
+    def _():
+        pl.semaphore_signal(barrier, inc=1, device_id=(g - 2, q), device_id_type=MESH)
+
+    @pl.when(line < last)
+    def _():
+        pl.semaphore_signal(barrier, inc=1, device_id=(g + 2, q), device_id_type=MESH)
+
+    ends = jnp.minimum(line, 1) + jnp.minimum(last - line, 1)
+    return lambda: pl.semaphore_wait(barrier, len(others) + 1 + ends)
+
+
+def all_in(ng, g, q, up, down):
+    line, last = g // 2, ng // 2 - 1
+
+    @pl.when(line == last)
+    def _():
+        @pl.when(line > 0)
+        def _():
+            pl.semaphore_signal(down, inc=1, device_id=(g - 2, q), device_id_type=MESH)
+
+    @pl.when(line > 0)
+    def _():
+        pl.semaphore_wait(up, 1)
+
+    @pl.when(line < last)
+    def _():
+        pl.semaphore_signal(up, inc=1, device_id=(g + 2, q), device_id_type=MESH)
+        pl.semaphore_wait(down, 1)
+
+        @pl.when(line > 0)
+        def _():
+            pl.semaphore_signal(down, inc=1, device_id=(g - 2, q), device_id_type=MESH)
+
+
 def gather_kernel(
     ng,
     feat,
@@ -81,12 +124,14 @@
     mask,
     pairs,
     degree,
+    adj,
     tcount,
+    tiles,
     fbuf,
     enc,
     table,
     wtrans,
-    hot,
+    srow,
     marks,
     inverse,
     lists,
@@ -100,7 +145,11 @@
     wmsg,
     pmsg,
     wbuf,
+    hot,
+    up,
+    down,
     local_sem,
+    tile_sem,
     small_sem,
     mark_sem,
     ws_core,
@@ -142,16 +191,7 @@
     for copy in small:
         copy.start()
 
-    barrier = pltpu.get_barrier_semaphore()
-    pl.semaphore_signal(barrier, inc=1, device_id=(g, across), device_id_type=MESH)
-    pl.semaphore_signal(barrier, inc=1, device_id=(g, partner), device_id_type=MESH)
-
-    def greet(d, c):
-        pl.semaphore_signal(barrier, inc=1, device_id=((g + d) % ng, q), device_id_type=MESH)
-        return c
-
-    lax.fori_loop(1, ng, greet, 0)
-
+    entered = enter(ng, g, q, (across, partner))
     for copy in small:
         copy.wait()
     for j in range(PR):
@@ -162,7 +202,7 @@
         other = pltpu.roll(turned, width, 1)
         wmsg[j] = jnp.where(k == 0, turned, other)[:sp].astype(bf16)
     marks[x] = jnp.where(msk[...] > 0, lab[...], -1)
-    pl.semaphore_wait(barrier, ng + 1)
+    entered()
 
     first = remote(wmsg, pmsg, ws_core.at[0], ws_core.at[1], (g, partner))
     first.start()
@@ -185,6 +225,9 @@
         return c
 
     lax.fori_loop(1, blocks, cross_all, 0)
+    fetch = pltpu.make_async_copy(adj, tiles, tile_sem)
+    fetch.start()
+    all_in(ng, g, q, up, down)
     second.wait()
 
     def to_group(d):
@@ -271,6 +314,7 @@
     line = lax.broadcasted_iota(jnp.int32, (TROWS, lanes), 0)
     for j in range(PR):
         at = jnp.where(flat >= 0, flat * PR + j, -1)
+        srow[:, j * lanes : (j + 1) * lanes] = at
         hot[:, j * lanes : (j + 1) * lanes] = (line == at).astype(f32).astype(bf16)
 
     def pass_on(d, c):
@@ -293,47 +337,47 @@
     for i in range(3):
         wtrans[i] = jnp.transpose(full[i * B : (i + 1) * B]).astype(bf16)
     bias = column_of(table[PROWS - 2 : PROWS + 14], 0)
-    bias = jnp.concatenate([bias] * 4, axis=1)
 
     def share(i, core):
-        away = i // (blocks // 2)
+        away = i // blocks
         quarter = (x + away * (1 - 2 * x)) * 2 + core
-        piece = enc.at[pl.ds(quarter * blocks + (i % (blocks // 2)) * 2, 2)]
+        piece = enc.at[quarter * blocks + i % blocks]
         return remote(piece, piece, en_send.at[i], en_recv.at[i], (g, partner))
 
-    def encode(i):
-        away = i // (blocks // 2)
+    def encode(i, many):
+        away = i // blocks
         side = x + away * (1 - 2 * x)
-        base = (i % (blocks // 2)) * 2
-        piece = fbuf[side, pl.ds(pl.multiple_of(base * B, 2 * B), 2 * B)]
-        pre = dot_nt(wtrans[0], piece) + bias
+        base = i % blocks
+        piece = fbuf[side, pl.ds(pl.multiple_of(base * B, B), many * B)]
+        pre = dot_nt(wtrans[0], piece) + jnp.concatenate([bias] * (2 * many), axis=1)
         out = (pre * sigmoid(pre)).astype(bf16)
         at = (side * 2 + k) * blocks + base
-        enc[at] = out[:, :B]
-        enc[at + 1] = out[:, B:]
-        share(i, k).start()
+        for n in range(many):
+            enc[at + n] = out[:, n * B : (n + 1) * B]
+        for n in range(many):
+            share(i + n, k).start()
 
     def own(i, c):
-        encode(i)
-        return c
-
-    lax.fori_loop(0, blocks // 2, own, 0)
+        encode(i * 4, 4)
+        return c
+
+    lax.fori_loop(0, blocks // 4, own, 0)
 
     def crossed(i):
         piece = fbuf.at[1 - x, pl.ds(pl.multiple_of(i * B, B), B)]
         return remote(piece, piece, xs_send.at[i], xs_recv.at[i], (g, across))
 
-    def far(i, c):
-        crossed(2 * i).wait_recv()
-        crossed(2 * i + 1).wait_recv()
-        encode(blocks // 2 + i)
-        return c
-
-    lax.fori_loop(0, blocks // 2, far, 0)
+    def far_block(i, c):
+        crossed(i).wait_recv()
+        encode(blocks + i, 1)
+        return c
+
+    lax.fori_loop(0, blocks, far_block, 0)
 
     def settle(i, c):
-        share(i, 1 - k).wait_recv()
-        share(i, k).wait_send()
+        for n in (i, blocks + i):
+            share(n, 1 - k).wait_recv()
+            share(n, k).wait_send()
         cross(i).wait_send()
         return c
 
@@ -348,59 +392,31 @@
     lax.fori_loop(1, ng, drain_group, 0)
     hand_over(0).wait_send()
     put.wait()
-
-
-RING = 32
-
-
-def each_tile(tiles, order, count, ring, sems, use):
-    def fetch(j):
-        return pltpu.make_async_copy(tiles.at[order(j)], ring.at[j % RING], sems.at[j % RING])
-
-    def ask(j):
-        @pl.when(j < count)
-        def _():
-            fetch(j).start()
-
-    def first(j, c):
-        ask(j)
-        return c
-
-    lax.fori_loop(0, RING, first, 0)
-
+    fetch.wait()
+
+
+def each_tile(count, use):
     def step(i, c):
         for u in range(UNROLL):
-            j = i * UNROLL + u
-
-            @pl.when(j < count)
-            def _():
-                fetch(j).wait()
-
-        for u in range(UNROLL):
-            j = i * UNROLL + u
-            use(j, ring[j % RING])
-        for u in range(UNROLL):
-            ask(i * UNROLL + u + RING)
-        return c
-
-    return lambda: lax.fori_loop(0, (count + UNROLL - 1) // UNROLL, step, 0)
-
-
-def forward_kernel(lists, tiles, enc, inverse, mean, acc, ring, sems):
+            use(i * UNROLL + u)
+        return c
+
+    lax.fori_loop(0, (count + UNROLL - 1) // UNROLL, step, 0)
+
+
+def forward_kernel(lists, tiles, enc, inverse, mean, acc):
     local = mean.shape[0]
     blocks = local // 2
 
-    def use(j, tile):
-        acc[lists[1, j]] += dot_nt(enc[lists[2, j]], tile)
-
-    run = each_tile(tiles, lambda j: lists[0, j], lists[6, 0], ring, sems, use)
+    def use(j):
+        acc[lists[1, j]] += dot_nt(enc[lists[2, j]], tiles[lists[0, j]])
 
     def clear(i, c):
         acc[i] = jnp.zeros((B, B), f32)
         return c
 
     lax.fori_loop(0, local + 1, clear, 0)
-    run()
+    each_tile(lists[6, 0], use)
 
     def finish(i, c):
         scale = inverse[i // blocks, :, pl.ds(pl.multiple_of((i % blocks) * B, B), B)]
@@ -488,7 +504,7 @@
             lanes = slice(b * B, (b + 1) * B)
             sums[at + b] = out[:, lanes]
             sage[2 * i + b] = sgrad[:, lanes]
-            hid[2 * i + b] = hidden[:, lanes]
+            hid[2 * i + b] = jnp.where(x == 0, hidden[:HALF, lanes], hidden[HALF:, lanes])
             lgrad[2 * i + b] = grad[:, lanes]
         exchange(i, k).start()
         return c
@@ -502,7 +518,7 @@
         s = sage[b, half]
         t1 = dot_nt(s, enc[at])
         t2 = dot_nt(s, mean[b])
-        t3 = dot_nt(lgrad[b], hid[b, half])
+        t3 = dot_nt(lgrad[b], hid[b])
         t4 = dot_nn(s, ones)
         sg = t1 if sg is None else sg + t1
         ng_ = t2 if ng_ is None else ng_ + t2
@@ -522,22 +538,20 @@
     lax.fori_loop(0, steps, done, 0)
 
 
-def backward_kernel(lists, tiles, sums, self_back, fbuf, table, wtrans, enc_grad, bias_grad, acc, ring, sems):
+def backward_kernel(lists, tiles, sums, self_back, fbuf, table, wtrans, enc_grad, bias_grad, acc):
     x = lax.axis_index("col") // 2
     local = self_back.shape[0]
     blocks = local // 2
 
-    def use(j, tile):
-        acc[lists[4, j]] += dot_nn(sums[lists[5, j]], tile)
-
-    run = each_tile(tiles, lambda j: lists[3, j], lists[7, 0], ring, sems, use)
+    def use(j):
+        acc[lists[4, j]] += dot_nn(sums[lists[5, j]], tiles[lists[3, j]])
 
     def clear(i, c):
         acc[i] = jnp.zeros((HALF, B), f32)
         return c
 
     lax.fori_loop(0, local + 1, clear, 0)
-    run()
+    each_tile(lists[7, 0], use)
     half = pl.ds(pl.multiple_of(x * HALF, HALF), HALF)
     wide = column_of(table[PROWS - 2 : PROWS + 14, half], 0)
     wide = jnp.concatenate([wide, wide], axis=1)
@@ -565,18 +579,19 @@
     neigh_grad,
     head_grad,
     bsage_grad,
-    hot,
+    srow,
     stats,
     slot_grad,
     loss,
     gtab,
-    pbuf,
-    rbuf,
+    rtab,
     qbuf,
     inbox,
     sbuf,
     srecv,
     sbox,
+    up,
+    down,
     core_sem,
     stat_sem,
     g_send,
@@ -585,51 +600,55 @@
     s_recv,
 ):
     g, q, k, x, partner, across = place()
-    barrier = pltpu.get_barrier_semaphore()
-    pl.semaphore_signal(barrier, inc=1, device_id=(g, partner), device_id_type=MESH)
-
-    def greet(d, c):
-        pl.semaphore_signal(barrier, inc=1, device_id=((g + d) % ng, q), device_id_type=MESH)
-        return c
-
-    lax.fori_loop(1, ng, greet, 0)
+    entered = enter(ng, g, q, (partner,))
     sp = inbox.shape[1]
     slots = ng * sp
 
     both = jnp.sum(stats[...], axis=1, keepdims=True)
     sbuf[...] = jnp.broadcast_to(both, sbuf.shape)
-    gtab[0:B] = jnp.transpose(enc_grad[...])
-    gtab[B : 2 * B] = jnp.transpose(self_grad[...])
-    gtab[2 * B : 3 * B] = jnp.transpose(neigh_grad[...])
-    gtab[3 * B : 3 * B + CLS] = head_grad[...]
+    gtab[0:B] = jnp.transpose(enc_grad[...]).astype(bf16)
+    gtab[B : 2 * B] = jnp.transpose(self_grad[...]).astype(bf16)
+    gtab[2 * B : 3 * B] = jnp.transpose(neigh_grad[...]).astype(bf16)
+    gtab[3 * B : 3 * B + CLS] = head_grad[...].astype(bf16)
     tail = lax.broadcasted_iota(jnp.int32, (16, HALF), 0)
     row_one = jnp.sum(jnp.transpose(benc_grad[...]), axis=0, keepdims=True)
     row_two = jnp.transpose(bsage_grad[...])[0:1]
-    gtab[PROWS - 2 : PROWS + 14] = jnp.where(tail == 0, row_one, jnp.where(tail == 1, row_two, 0.0))
-    whole = gtab[...]
-    rolled = pltpu.roll(whole, HALF // 2, 1)
-    low = lax.broadcasted_iota(jnp.int32, (TROWS, HALF), 1) < HALF // 2
-
-    def spread(first, second):
-        one = jnp.where(low, first, 0.0).astype(bf16)
-        two = jnp.where(low, 0.0, second).astype(bf16)
-        both = dot_tn(hot[:, :slots], one) + dot_tn(hot[:, slots:], two)
-        return both.astype(bf16)
-
-    pbuf[0] = spread(whole, rolled)
-    pbuf[1] = spread(rolled, whole)
-    pl.semaphore_wait(barrier, ng)
-
-    one = remote(pbuf.at[1 - k], rbuf, core_sem.at[0], core_sem.at[1], (g, partner))
+    last = jnp.where(tail == 0, row_one, jnp.where(tail == 1, row_two, 0.0))
+    gtab[PROWS - 2 : PROWS + 14] = last.astype(bf16)
+    entered()
+    one = remote(gtab, rtab, core_sem.at[0], core_sem.at[1], (g, partner))
     one.start()
     two = remote(sbuf, srecv, stat_sem.at[0], stat_sem.at[1], (g, partner))
     two.start()
+    all_in(ng, g, q, up, down)
     one.wait()
     two.wait()
-    qbuf[...] = (
-        (pbuf[k].astype(f32) + rbuf[...].astype(f32)).astype(bf16).reshape(ng, sp, HALF)
-    )
     sbox[g] = sbuf[...] + srecv[...]
+
+    def stat_out(d):
+        to = (g + d) % ng
+        return remote(sbox.at[g], sbox.at[g], s_send.at[d], s_recv.at[d], (to, q))
+
+    def stat_got(d):
+        src = (g + ng - d) % ng
+        return remote(sbox.at[src], sbox.at[src], s_send.at[d], s_recv.at[d], (src, q))
+
+    def start_stat(d, c):
+        stat_out(d).start()
+        return c
+
+    lax.fori_loop(1, ng, start_stat, 0)
+
+    whole = gtab[...].astype(f32) + rtab[...].astype(f32)
+    rolled = pltpu.roll(whole, HALF // 2, 1)
+    low = lax.broadcasted_iota(jnp.int32, (TROWS, HALF), 1) < HALF // 2
+    line = lax.broadcasted_iota(jnp.int32, (TROWS, slots), 0)
+    even = jnp.where(low, jnp.where(k == 0, whole, rolled), 0.0).astype(bf16)
+    odd = jnp.where(low, 0.0, jnp.where(k == 0, rolled, whole)).astype(bf16)
+    hot_even = (line == srow[:, :slots]).astype(f32).astype(bf16)
+    hot_odd = (line == srow[:, slots:]).astype(f32).astype(bf16)
+    spread = dot_tn(hot_even, even) + dot_tn(hot_odd, odd)
+    qbuf[...] = spread.astype(bf16).reshape(ng, sp, HALF)
 
     def out(d):
         to = (g + d) % ng
@@ -639,16 +658,7 @@
         src = (g + ng - d) % ng
         return remote(qbuf.at[src], inbox.at[src], g_send.at[d], g_recv.at[d], (src, q))
 
-    def stat_out(d):
-        to = (g + d) % ng
-        return remote(sbox.at[g], sbox.at[g], s_send.at[d], s_recv.at[d], (to, q))
-
-    def stat_got(d):
-        src = (g + ng - d) % ng
-        return remote(sbox.at[src], sbox.at[src], s_send.at[d], s_recv.at[d], (src, q))
-
     def start(d, c):
-        stat_out(d).start()
         out(d).start()
         return c
 
@@ -753,20 +763,21 @@
     first_t = jnp.transpose(moment_one, (1, 2, 0))
     second_t = jnp.transpose(moment_two, (1, 2, 0))
 
-    fbuf, enc, table, wtrans, hot, marks, inverse, lists = pl.pallas_call(
+    tiles, fbuf, enc, table, wtrans, srow, marks, inverse, lists = pl.pallas_call(
         functools.partial(gather_kernel, ng),
         out_shape=(
+            pltpu.VMEM((count, B, B), bf16),
             pltpu.VMEM((2, rows, F), bf16),
             pltpu.VMEM((nb, HID, B), bf16),
             pltpu.VMEM((TROWS, HID), bf16),
             pltpu.VMEM((3, HID, HID), bf16),
-            pltpu.VMEM((TROWS, 2 * ng * sp), bf16),
+            pltpu.VMEM((1, 2 * ng * sp), jnp.int32),
             pltpu.VMEM((2, 1, rows), jnp.int32),
             pltpu.VMEM((2, 1, rows), f32),
             sds((8, tpad), jnp.int32),
         ),
-        in_specs=[HBM] * 7 + [SM],
-        out_specs=(VM,) * 7 + (HBM,),
+        in_specs=[HBM] * 8 + [SM],
+        out_specs=(VM,) * 8 + (HBM,),
         scratch_shapes=[
             pltpu.VMEM((PR, width, slots), f32),
             pltpu.VMEM((ng, slots), jnp.int32),
@@ -778,6 +789,10 @@
             pltpu.VMEM((2, sp, HALF), bf16),
             pltpu.VMEM((2, sp, HALF), bf16),
             pltpu.VMEM((2, ng, 2, sp, HALF), bf16),
+            pltpu.VMEM((TROWS, 2 * ng * sp), bf16),
+            pltpu.SemaphoreType.REGULAR,
+            pltpu.SemaphoreType.REGULAR,
+            DMA,
             DMA,
             DMA((7,)),
             DMA((2,)),
@@ -789,10 +804,10 @@
             DMA((ng,)),
             DMA((blocks,)),
             DMA((blocks,)),
-            DMA((blocks,)),
-            DMA((blocks,)),
+            DMA((2 * blocks,)),
+            DMA((2 * blocks,)),
         ],
-        compiler_params=params(12, 0),
+        compiler_params=params(6, 0),
         name="gather",
     )(
         far(features),
@@ -802,19 +817,19 @@
         far(loss_mask.reshape(1, rows)),
         far(jnp.transpose(block_pairs, (0, 2, 1))),
         far(degree.reshape(nc, 1, rows)),
+        far(adj_tiles),
         tile_count,
     )
 
-    adj = far(adj_tiles)
     mean = pl.pallas_call(
         forward_kernel,
         out_shape=pltpu.VMEM((local, HID, B), bf16),
-        in_specs=[SM, HBM, VM, VM],
+        in_specs=[SM, VM, VM, VM],
         out_specs=VM,
-        scratch_shapes=[pltpu.VMEM((local + 1, HID, B), f32), pltpu.VMEM((RING, B, B), bf16), DMA((RING,))],
-        compiler_params=params(14),
+        scratch_shapes=[pltpu.VMEM((local + 1, HID, B), f32)],
+        compiler_params=params(7),
         name="forward",
-    )(lists, adj, enc, inverse)
+    )(lists, tiles, enc, inverse)
 
     sums, self_back, self_grad, neigh_grad, head_grad, bsage, stats = pl.pallas_call(
         sage_kernel,
@@ -831,24 +846,24 @@
         out_specs=(VM,) * 7,
         scratch_shapes=[
             pltpu.VMEM((local, HID, B), bf16),
-            pltpu.VMEM((local, HID, B), bf16),
+            pltpu.VMEM((local, HALF, B), bf16),
             pltpu.VMEM((local, CLS, B), bf16),
             DMA((blocks,)),
             DMA((blocks,)),
         ],
-        compiler_params=params(12, 1),
+        compiler_params=params(8, 1),
         name="sage",
     )(enc, mean, table, wtrans, marks, inverse)
 
     enc_grad, benc = pl.pallas_call(
         backward_kernel,
         out_shape=(pltpu.VMEM((HALF, F), f32), pltpu.VMEM((HALF, HALF), f32)),
-        in_specs=[SM, HBM, VM, VM, VM, VM, VM],
+        in_specs=[SM, VM, VM, VM, VM, VM, VM],
         out_specs=(VM,) * 2,
-        scratch_shapes=[pltpu.VMEM((local + 1, HALF, B), f32), pltpu.VMEM((RING, B, B), bf16), DMA((RING,))],
-        compiler_params=params(12),
+        scratch_shapes=[pltpu.VMEM((local + 1, HALF, B), f32)],
+        compiler_params=params(6),
         name="backward",
-    )(lists, adj, sums, self_back, fbuf, table, wtrans)
+    )(lists, tiles, sums, self_back, fbuf, table, wtrans)
 
     packed, loss = pl.pallas_call(
         functools.partial(reduce_kernel, ng),
@@ -856,14 +871,15 @@
         in_specs=[VM] * 8,
         out_specs=(VM,) * 2,
         scratch_shapes=[
-            pltpu.VMEM((TROWS, HALF), f32),
-            pltpu.VMEM((2, ng * sp, HALF), bf16),
-            pltpu.VMEM((ng * sp, HALF), bf16),
+            pltpu.VMEM((TROWS, HALF), bf16),
+            pltpu.VMEM((TROWS, HALF), bf16),
             pltpu.VMEM((ng, sp, HALF), bf16),
             pltpu.VMEM((ng, sp, HALF), bf16),
             pltpu.VMEM((8, HALF), f32),
             pltpu.VMEM((8, HALF), f32),
             pltpu.VMEM((ng, 8, HALF), f32),
+            pltpu.SemaphoreType.REGULAR,
+            pltpu.SemaphoreType.REGULAR,
             DMA((2,)),
             DMA((2,)),
             DMA((ng,)),
@@ -873,7 +889,7 @@
         ],
         compiler_params=params(12, 2),
         name="reduce",
-    )(enc_grad, benc, self_grad, neigh_grad, head_grad, bsage, hot, stats)
+    )(enc_grad, benc, self_grad, neigh_grad, head_grad, bsage, srow, stats)
 
     shape = (PR, width, slots)
     new_master, new_first, new_second, low, mean_loss = pl.pallas_call(

time: 72.7 us -> 68.7 us (0.945)
  Pallas kernels: 70.5 us -> 66.7 us
    pallas_call x1, Pallas kernels: 9.45 us -> 14.4 us  [body(): pl.pallas_call(functools.partial(reduce_kernel, ng), out_shape=(pltpu.VME...]
    pallas_call x1, Pallas kernels: 8.9 us -> 5.68 us  [body(): pl.pallas_call(forward_kernel, out_shape=pltpu.VMEM((local, HID, B), bf16...]
    pallas_call x1, Pallas kernels: 33.2 us -> 30.2 us  [body(): pl.pallas_call(functools.partial(gather_kernel, ng), out_shape=(pltpu.VME...]
    pallas_call x1, Pallas kernels: 8.19 us -> 5.22 us  [body(): pl.pallas_call(backward_kernel, out_shape=(pltpu.VMEM((HALF, F), f32), pl...]
where the time goes in v3:
time: 68.7 us; the launch traced here: 68.1 us
  Pallas kernels  66.7 us (97%)
  between operations  1.38 us (2%)
    pallas_call x1, Pallas kernels, body(): pl.pallas_call(functools.partial(gather_kernel, ng), out_shape=(pltpu.VME...  30.2 us
    pallas_call x1, Pallas kernels, body(): pl.pallas_call(functools.partial(reduce_kernel, ng), out_shape=(pltpu.VME...  14.4 us
    pallas_call x1, Pallas kernels, body(): pl.pallas_call(sage_kernel, out_shape=(pltpu.VMEM((nb, HALF, B), bf16), p...  10.3 us
    pallas_call x1, Pallas kernels, body(): pl.pallas_call(forward_kernel, out_shape=pltpu.VMEM((local, HID, B), bf16...  5.68 us
    pallas_call x1, Pallas kernels, body(): pl.pallas_call(backward_kernel, out_shape=(pltpu.VMEM((HALF, F), f32), pl...  5.22 us

profile of v3, /device:TPU:0, one launch (start us, length us, event | category | flops | bytes accessed | tf_op | source)
XLA Modules:
  0.0 68.1 jit_solution(4349107146828745743)
XLA Ops:
  1.3 30.2 %gather.1 = (bf16[192,256,256]{2,1,0:T(8,128)(2,1)S(1)}, bf16[2,2048,256]{2,1,0:T(8,128)(2,1)S(1)}, bf16[32,256,256]{2,1,0:T(8,128)(2,1)S(1)}, bf16[848,256]{1,0...) custom-call(bf16[2048,256]{1,0:T(8,128)(2,1)} %feat.1, ...), custom_call_target="tpu_custom_call" | custom-call | tf_op jit(solution)/shard_map/gather/pallas_call | solution.py:766
  31.5 5.7 %forward.1.mean = bf16[16,256,256]{2,1,0:T(8,128)(2,1)S(1)} custom-call(s32[8,256]{1,0:T(8,128)S(1)} %get-tuple-element.30.lists, bf16[192,256,256]{2,1,0:T(8,128)(2,1)S(1)} %get-tuple-element.31.tiles, bf16[32,256,256]{2,1,0:T(8,128)(2,1)S(1)} %get-tuple-element.32.enc, f32[2,1,2048]{2,1,0:T(1,128)S(1)} %get-tuple-element.33.inverse), custom_call_target="tpu_custom_call" | custom-call | tf_op jit(solution)/shard_map/forward/pallas_call | solution.py:824
  37.2 10.3 %sage.1 = (bf16[32,128,256]{2,1,0:T(8,128)(2,1)S(1)}, f32[16,128,256]{2,1,0:T(8,128)S(1)}, f32[128,256]{1,0:T(8,128)S(1)}, f32[128,256]{1,0:T(8,128)S(1)}, f32[6...) custom-call(bf16[32,256,256]{2,1,0:T(8,128)(2,1)S(1)} %get-tuple-element.32.enc, ...), custom_call_target="tpu_custom_call" | custom-call | tf_op jit(solution)/shard_map/sage/pallas_call | solution.py:834
  47.5 0.0 copy-start
  47.5 0.0 copy-start.1
  47.5 0.0 copy-start.2
  47.6 0.0 copy-start.3
  47.6 5.2 %backward.1 = (f32[128,256]{1,0:T(8,128)S(1)}, f32[128,128]{1,0:T(8,128)S(1)}) custom-call(s32[8,256]{1,0:T(8,128)S(1)} %get-tuple-element.30.lists, bf16[192,256,256]{2,1,0:T(8,128)(2,1)S(1)} %get-tuple-element.31.tiles, bf16[32,128,256]{2,1,0:T(8,128)(2,1)S(1)} %get-tuple-element.37.sums, f32[16,128,256]{2,1,0:T(8,128)S(1)} %get-tuple-element.38.self_back, ...), custom_call_target="tpu_custom_call" | custom-call | tf_op jit(solution)/shard_map/backward/pallas_call | solution.py:858
  52.8 14.4 %reduce.1 = (f32[80,128]{1,0:T(8,128)S(1)}, f32[8,128]{1,0:T(8,128)S(1)}) custom-call(f32[128,256]{1,0:T(8,128)S(1)} %get-tuple-element.40.enc_grad, f32[128,128]{1,0:T(8,128)S(1)} %get-tuple-element.41.benc_grad, f32[128,256]{1,0:T(8,128)S(1)} %get-tuple-element.42.self_grad, f32[128,256]{1,0:T(8,128)S(1)} %get-tuple-element.43.neigh_grad, ...), custom_call_target="tpu_custom_call" | custom-call | tf_op jit(solution)/shard_map/reduce/pallas_call | solution.py:868
  67.2 0.0 copy-done
  67.2 0.0 copy-done.1
  67.2 0.0 copy-done.2
  67.3 0.0 copy-done.3
  67.3 0.8 %update.1 = (f32[2,64,79]{2,1,0:T(8,128)}, f32[2,64,79]{2,1,0:T(8,128)}, f32[2,64,79]{2,1,0:T(8,128)}, bf16[2,64,79]{2,1,0:T(8,128)(2,1)}, f32[1,1]{1,0:T(1,128)}) custom-call(f32[80,128]{1,0:T(8,128)S(1)} %get-tuple-element.48.packed, f32[8,128]{1,0:T(8,128)S(1)} %get-tuple-element.49.loss, s32[8,79]{1,0:T(8,128)S(1)} %copy-done.3, ...), custom_call_target="tpu_custom_call" | custom-call | tf_op jit(solution)/shard_map/update/pallas_call | solution.py:895
Async XLA Ops:
  47.5 19.7 %copy-start = (f32[79,2,64]{0,2,1:T(8,128)S(1)}, f32[79,2,64]{0,2,1:T(8,128)}, u32[]{:S(2)}) copy-start(f32[79,2,64]{0,2,1:T(8,128)} %param.19) | copy-start | bytes 121348
  47.5 19.7 %copy-start.1 = (f32[79,2,64]{0,2,1:T(8,128)S(1)}, f32[79,2,64]{0,2,1:T(8,128)}, u32[]{:S(2)}) copy-start(f32[79,2,64]{0,2,1:T(8,128)} %param.20) | copy-start | bytes 121348
  47.5 19.7 %copy-start.2 = (f32[79,2,64]{0,2,1:T(8,128)S(1)}, f32[79,2,64]{0,2,1:T(8,128)}, u32[]{:S(2)}) copy-start(f32[79,2,64]{0,2,1:T(8,128)} %param.21) | copy-start | bytes 121348
  47.6 19.7 %copy-start.3 = (s32[8,79]{1,0:T(8,128)S(1)}, s32[8,79]{1,0:T(8,128)}, u32[]{:S(2)}) copy-start(s32[8,79]{1,0:T(8,128)} %pieces.3) | copy-start | bytes 7588

commit v4 on v3

--- a/solution.py
+++ b/solution.py
@@ -15,7 +15,7 @@
 PROWS = 834
 TROWS = 848
 HALF = 128
-UNROLL = 8
+WIDE = 8
 
 learn_rate = 0.01
 beta_one = 0.5
@@ -149,6 +149,7 @@
     up,
     down,
     local_sem,
+    put_sem,
     tile_sem,
     small_sem,
     mark_sem,
@@ -192,6 +193,13 @@
         copy.start()
 
     entered = enter(ng, g, q, (across, partner))
+    def cross(i):
+        at = pl.ds(pl.multiple_of(i * B, B), B)
+        return remote(feat.at[at], fbuf.at[x, at], xs_send.at[i], xs_recv.at[i], (g, across))
+
+    entered()
+    cross(0).start()
+    cross(1).start()
     for copy in small:
         copy.wait()
     for j in range(PR):
@@ -201,20 +209,11 @@
         turned = jnp.transpose(jnp.concatenate([cols, jnp.zeros_like(cols)], axis=0))
         other = pltpu.roll(turned, width, 1)
         wmsg[j] = jnp.where(k == 0, turned, other)[:sp].astype(bf16)
-    marks[x] = jnp.where(msk[...] > 0, lab[...], -1)
-    entered()
-
     first = remote(wmsg, pmsg, ws_core.at[0], ws_core.at[1], (g, partner))
     first.start()
+    marks[x] = jnp.where(msk[...] > 0, lab[...], -1)
     mark_copy = remote(marks.at[x], marks.at[x], mark_sem.at[0], mark_sem.at[1], (g, across))
     mark_copy.start()
-    load.wait()
-
-    def cross(i):
-        piece = fbuf.at[x, pl.ds(pl.multiple_of(i * B, B), B)]
-        return remote(piece, piece, xs_send.at[i], xs_recv.at[i], (g, across))
-
-    cross(0).start()
     first.wait()
     wbuf[k, g, x] = wmsg[k] + pmsg[k]
     second = remote(wbuf.at[k, g, x], wbuf.at[k, g, x], ws_x.at[0], ws_x.at[1], (g, across))
@@ -224,7 +223,7 @@
         cross(i).start()
         return c
 
-    lax.fori_loop(1, blocks, cross_all, 0)
+    lax.fori_loop(2, blocks, cross_all, 0)
     fetch = pltpu.make_async_copy(adj, tiles, tile_sem)
     fetch.start()
     all_in(ng, g, q, up, down)
@@ -296,7 +295,7 @@
     ft, fr, fc, fn = compact(fmine, frow, cvec)
     bt, bc, br, bn = compact(bmine, bcol, rvec)
     lbuf[...] = jnp.concatenate([ft, fr, fc, bt, bc, br, fn, bn], axis=0)
-    put = pltpu.make_async_copy(lbuf, lists, local_sem)
+    put = pltpu.make_async_copy(lbuf, lists, put_sem)
     put.start()
     inverse[...] = 1.0 / deg[...].astype(f32)
 
@@ -357,6 +356,8 @@
         for n in range(many):
             share(i + n, k).start()
 
+    load.wait()
+
     def own(i, c):
         encode(i * 4, 4)
         return c
@@ -364,8 +365,8 @@
     lax.fori_loop(0, blocks // 4, own, 0)
 
     def crossed(i):
-        piece = fbuf.at[1 - x, pl.ds(pl.multiple_of(i * B, B), B)]
-        return remote(piece, piece, xs_send.at[i], xs_recv.at[i], (g, across))
+        at = pl.ds(pl.multiple_of(i * B, B), B)
+        return remote(feat.at[at], fbuf.at[1 - x, at], xs_send.at[i], xs_recv.at[i], (g, across))
 
     def far_block(i, c):
         crossed(i).wait_recv()
@@ -396,12 +397,21 @@
 
 
 def each_tile(count, use):
-    def step(i, c):
-        for u in range(UNROLL):
-            use(i * UNROLL + u)
-        return c
-
-    lax.fori_loop(0, (count + UNROLL - 1) // UNROLL, step, 0)
+    def many(i, c):
+        for u in range(32):
+            use(i * 32 + u)
+        return c
+
+    whole = count // 32
+    lax.fori_loop(0, whole, many, 0)
+    done = whole * 32
+
+    def few(i, c):
+        for u in range(8):
+            use(done + i * 8 + u)
+        return c
+
+    lax.fori_loop(0, (count - done + 7) // 8, few, 0)
 
 
 def forward_kernel(lists, tiles, enc, inverse, mean, acc):
@@ -450,92 +460,105 @@
     local = mean.shape[0]
     blocks = local // 2
     width = 2 * B
-    steps = local // 2
+    steps = local // WIDE
+    side = steps // 2
     barrier = pltpu.get_barrier_semaphore()
     pl.semaphore_signal(barrier, inc=1, device_id=(g, partner), device_id_type=MESH)
-    pl.semaphore_wait(barrier, 1)
-    half = pl.ds(pl.multiple_of(x * HALF, HALF), HALF)
     head = table[F + 2 * HID : F + 2 * HID + CLS]
     bias = column_of(table[PROWS - 2 : PROWS + 14], 1)
     bias = jnp.concatenate([bias] * 4, axis=1)
-    neigh_half = table[pl.ds(pl.multiple_of(F + HID + x * HALF, HALF), HALF)]
-    self_half = table[pl.ds(pl.multiple_of(F + x * HALF, HALF), HALF)]
-    stats[...] = jnp.zeros_like(stats)
+    both_half = jnp.concatenate(
+        [
+            table[pl.ds(pl.multiple_of(F + HID + x * HALF, HALF), HALF)],
+            table[pl.ds(pl.multiple_of(F + x * HALF, HALF), HALF)],
+        ],
+        axis=0,
+    )
 
     def slot(i, core):
-        return (i // (steps // 2)) * 2 * blocks + core * blocks + (i % (steps // 2)) * 2
+        return (i // side) * 2 * blocks + core * blocks + (i % side) * WIDE
 
     def exchange(i, core):
-        piece = sums.at[pl.ds(slot(i, core), 2)]
-        return pltpu.make_async_remote_copy(
-            src_ref=piece,
-            dst_ref=piece,
-            send_sem=send.at[i],
-            recv_sem=recv.at[i],
-            device_id=(g, partner),
-            device_id_type=MESH,
-        )
-
-    def step(i, c):
+        piece = sums.at[pl.ds(slot(i, core), WIDE)]
+        return remote(piece, piece, send.at[i], recv.at[i], (g, partner))
+
+    loss_rows = jnp.zeros((1, width), f32)
+    valid_rows = jnp.zeros((1, width), f32)
+    bias_sum = jnp.zeros((HALF, HALF), f32)
+    parts = range(WIDE // 2)
+    grads = []
+
+    def weight_grads(i):
+        total = [None, None, None]
+        for b in range(WIDE):
+            n = i * WIDE + b
+            here = (
+                dot_nt(sage[n], enc[slot(i, k) + b]),
+                dot_nt(sage[n], mean[n]),
+                dot_nt(lgrad[n], hid[n]),
+            )
+            total = [h if t is None else t + h for t, h in zip(total, here)]
+        for ref, t in zip((self_grad, neigh_grad, head_grad), total):
+            ref[...] = t if i == 0 else ref[...] + t
+
+    for i in range(steps):
         at = slot(i, k)
-        e = jnp.concatenate([enc[at], enc[at + 1]], axis=1)
-        m = jnp.concatenate([mean[2 * i], mean[2 * i + 1]], axis=1)
-        pre = dot_nn(wtrans[1], e) + dot_nn(wtrans[2], m) + bias
-        sig = sigmoid(pre)
-        hidden = (pre * sig).astype(bf16)
-        logits = dot_nn(head, hidden)
-        top = jnp.max(logits, axis=0, keepdims=True)
-        expd = jnp.exp(logits - top)
-        total = jnp.sum(expd, axis=0, keepdims=True)
-        cols = pl.ds(pl.multiple_of((i % (steps // 2)) * width, width), width)
-        mark = marks[i // (steps // 2), :, cols]
-        valid = (mark >= 0).astype(f32)
-        onehot = (lax.broadcasted_iota(jnp.int32, (CLS, width), 0) == mark).astype(f32)
-        target = jnp.sum(logits * onehot, axis=0, keepdims=True)
-        loss = valid * (top + jnp.log(total) - target)
-        stats[0:1, :] += loss
-        stats[1:2, :] += valid
-        grad = ((expd * (1.0 / total) - onehot) * valid).astype(bf16)
-        back = dot_tn(head, grad) * (sig * (1.0 + pre * (1.0 - sig)))
-        sgrad = back.astype(bf16)
-        scale = inverse[i // (steps // 2), :, cols]
-        out = (dot_nn(neigh_half, sgrad) * scale).astype(bf16)
-        for b in range(2):
-            lanes = slice(b * B, (b + 1) * B)
-            sums[at + b] = out[:, lanes]
-            sage[2 * i + b] = sgrad[:, lanes]
-            hid[2 * i + b] = jnp.where(x == 0, hidden[:HALF, lanes], hidden[HALF:, lanes])
-            lgrad[2 * i + b] = grad[:, lanes]
+        pre, sig, hidden, grad = {}, {}, {}, {}
+        for p in parts:
+            e = jnp.concatenate([enc[at + 2 * p], enc[at + 2 * p + 1]], axis=1)
+            n = i * WIDE + 2 * p
+            m = jnp.concatenate([mean[n], mean[n + 1]], axis=1)
+            pre[p] = dot_nn(wtrans[1], e) + dot_nn(wtrans[2], m) + bias
+        for p in parts:
+            sig[p] = sigmoid(pre[p])
+            hidden[p] = (pre[p] * sig[p]).astype(bf16)
+        if i > 0:
+            weight_grads(i - 1)
+        for p in parts:
+            logits = dot_nn(head, hidden[p])
+            top = jnp.max(logits, axis=0, keepdims=True)
+            expd = jnp.exp(logits - top)
+            total = jnp.sum(expd, axis=0, keepdims=True)
+            base = (i % side) * WIDE * B + p * width
+            mark = marks[i // side, :, base : base + width]
+            valid = (mark >= 0).astype(f32)
+            hot = lax.broadcasted_iota(jnp.int32, (CLS, width), 0) == mark
+            onehot = hot.astype(f32)
+            target = jnp.sum(logits * onehot, axis=0, keepdims=True)
+            loss_rows = loss_rows + valid * (top + jnp.log(total) - target)
+            valid_rows = valid_rows + valid
+            grad[p] = ((expd * (1.0 / total) - onehot) * valid).astype(bf16)
+        outs = {}
+        for p in parts:
+            back = dot_tn(head, grad[p]) * (sig[p] * (1.0 + pre[p] * (1.0 - sig[p])))
+            sgrad = back.astype(bf16)
+            base = (i % side) * WIDE * B + p * width
+            outs[p] = dot_nn(both_half, sgrad)
+            scale = inverse[i // side, :, base : base + width]
+            out = (outs[p][:HALF] * scale).astype(bf16)
+            mine = jnp.where(x == 0, sgrad[:HALF], sgrad[HALF:])
+            own = jnp.where(x == 0, hidden[p][:HALF], hidden[p][HALF:])
+            fine = mine.astype(f32)
+            for v in range(4):
+                bias_sum = bias_sum + fine[:, v * HALF : (v + 1) * HALF]
+            for b in range(2):
+                lanes = slice(b * B, (b + 1) * B)
+                n = i * WIDE + 2 * p + b
+                sums[at + 2 * p + b] = out[:, lanes]
+                self_back[n] = outs[p][HALF:, lanes]
+                sage[n] = mine[:, lanes]
+                hid[n] = own[:, lanes]
+                lgrad[n] = grad[p][:, lanes]
+        if i == 0:
+            pl.semaphore_wait(barrier, 1)
         exchange(i, k).start()
-        return c
-
-    lax.fori_loop(0, steps, step, 0)
-
-    ones = jnp.ones((B, HALF), bf16)
-    sg = ng_ = hg = bg = None
-    for b in range(local):
-        at = (b // blocks) * 2 * blocks + k * blocks + b % blocks
-        s = sage[b, half]
-        t1 = dot_nt(s, enc[at])
-        t2 = dot_nt(s, mean[b])
-        t3 = dot_nt(lgrad[b], hid[b])
-        t4 = dot_nn(s, ones)
-        sg = t1 if sg is None else sg + t1
-        ng_ = t2 if ng_ is None else ng_ + t2
-        hg = t3 if hg is None else hg + t3
-        bg = t4 if bg is None else bg + t4
-        self_back[b] = dot_nn(self_half, sage[b])
-    self_grad[...] = sg
-    neigh_grad[...] = ng_
-    head_grad[...] = hg
-    bias_grad[...] = bg
-
-    def done(i, c):
+
+    weight_grads(steps - 1)
+    bias_grad[...] = bias_sum
+    stats[...] = jnp.concatenate([loss_rows, valid_rows, jnp.zeros((6, width), f32)], axis=0)
+    for i in range(steps):
         exchange(i, 1 - k).wait_recv()
         exchange(i, k).wait_send()
-        return c
-
-    lax.fori_loop(0, steps, done, 0)
 
 
 def backward_kernel(lists, tiles, sums, self_back, fbuf, table, wtrans, enc_grad, bias_grad, acc):
@@ -612,7 +635,7 @@
     gtab[3 * B : 3 * B + CLS] = head_grad[...].astype(bf16)
     tail = lax.broadcasted_iota(jnp.int32, (16, HALF), 0)
     row_one = jnp.sum(jnp.transpose(benc_grad[...]), axis=0, keepdims=True)
-    row_two = jnp.transpose(bsage_grad[...])[0:1]
+    row_two = jnp.sum(jnp.transpose(bsage_grad[...]), axis=0, keepdims=True)
     last = jnp.where(tail == 0, row_one, jnp.where(tail == 1, row_two, 0.0))
     gtab[PROWS - 2 : PROWS + 14] = last.astype(bf16)
     entered()
@@ -774,10 +797,10 @@
             pltpu.VMEM((1, 2 * ng * sp), jnp.int32),
             pltpu.VMEM((2, 1, rows), jnp.int32),
             pltpu.VMEM((2, 1, rows), f32),
-            sds((8, tpad), jnp.int32),
+            pltpu.SMEM((8, tpad), jnp.int32),
         ),
         in_specs=[HBM] * 8 + [SM],
-        out_specs=(VM,) * 8 + (HBM,),
+        out_specs=(VM,) * 8 + (SM,),
         scratch_shapes=[
             pltpu.VMEM((PR, width, slots), f32),
             pltpu.VMEM((ng, slots), jnp.int32),
@@ -792,6 +815,7 @@
             pltpu.VMEM((TROWS, 2 * ng * sp), bf16),
             pltpu.SemaphoreType.REGULAR,
             pltpu.SemaphoreType.REGULAR,
+            DMA,
             DMA,
             DMA,
             DMA((7,)),
@@ -845,11 +869,11 @@
         in_specs=[VM] * 6,
         out_specs=(VM,) * 7,
         scratch_shapes=[
-            pltpu.VMEM((local, HID, B), bf16),
+            pltpu.VMEM((local, HALF, B), bf16),
             pltpu.VMEM((local, HALF, B), bf16),
             pltpu.VMEM((local, CLS, B), bf16),
-            DMA((blocks,)),
-            DMA((blocks,)),
+            DMA((local // WIDE,)),
+            DMA((local // WIDE,)),
         ],
         compiler_params=params(8, 1),
         name="sage",

time: 68.7 us -> 61.8 us (0.90); the launches traced: 68.1 us -> 62.2 us
  Pallas kernels: 66.7 us -> 60.7 us
    pallas_call x1, Pallas kernels: 10.3 us -> 7.06 us  [body(): pl.pallas_call(sage_kernel, out_shape=(pltpu.VMEM((nb, HALF, B), bf16), p...]
    pallas_call x1, Pallas kernels: 5.68 us -> 4.44 us  [body(): pl.pallas_call(forward_kernel, out_shape=pltpu.VMEM((local, HID, B), bf16...]
    pallas_call x1, Pallas kernels: 5.22 us -> 4.23 us  [body(): pl.pallas_call(backward_kernel, out_shape=(pltpu.VMEM((HALF, F), f32), pl...]
    pallas_call x1, Pallas kernels: 14.4 us -> 13.7 us  [body(): pl.pallas_call(functools.partial(reduce_kernel, ng), out_shape=(pltpu.VME...]
where the time goes in v4:
time: 61.8 us; the launch traced here: 62.2 us
  Pallas kernels  60.7 us (98%)
  between operations  1.54 us (2%)
    pallas_call x1, Pallas kernels, body(): pl.pallas_call(functools.partial(gather_kernel, ng), out_shape=(pltpu.VME...  30.4 us
    pallas_call x1, Pallas kernels, body(): pl.pallas_call(functools.partial(reduce_kernel, ng), out_shape=(pltpu.VME...  13.7 us
    pallas_call x1, Pallas kernels, body(): pl.pallas_call(sage_kernel, out_shape=(pltpu.VMEM((nb, HALF, B), bf16), p...  7.06 us
    pallas_call x1, Pallas kernels, body(): pl.pallas_call(forward_kernel, out_shape=pltpu.VMEM((local, HID, B), bf16...  4.44 us
    pallas_call x1, Pallas kernels, body(): pl.pallas_call(backward_kernel, out_shape=(pltpu.VMEM((HALF, F), f32), pl...  4.23 us

profile of v4, /device:TPU:0, one launch (start us, length us, event | category | flops | bytes accessed | tf_op | source)
XLA Modules:
  0.0 62.2 jit_solution(15286815744576061286)
XLA Ops:
  1.3 30.4 %gather.1 = (bf16[192,256,256]{2,1,0:T(8,128)(2,1)S(1)}, bf16[2,2048,256]{2,1,0:T(8,128)(2,1)S(1)}, bf16[32,256,256]{2,1,0:T(8,128)(2,1)S(1)}, bf16[848,256]{1,0...) custom-call(bf16[2048,256]{1,0:T(8,128)(2,1)} %feat.1, ...), custom_call_target="tpu_custom_call" | custom-call | tf_op jit(solution)/shard_map/gather/pallas_call | solution.py:789
  31.7 4.4 %forward.1.mean = bf16[16,256,256]{2,1,0:T(8,128)(2,1)S(1)} custom-call(s32[8,256]{1,0:T(8,128)S(4)} %get-tuple-element.30.lists, bf16[192,256,256]{2,1,0:T(8,128)(2,1)S(1)} %get-tuple-element.31.tiles, bf16[32,256,256]{2,1,0:T(8,128)(2,1)S(1)} %get-tuple-element.32.enc, f32[2,1,2048]{2,1,0:T(1,128)S(1)} %get-tuple-element.33.inverse), custom_call_target="tpu_custom_call" | custom-call | tf_op jit(solution)/shard_map/forward/pallas_call | solution.py:848
  36.2 7.1 %sage.1 = (bf16[32,128,256]{2,1,0:T(8,128)(2,1)S(1)}, f32[16,128,256]{2,1,0:T(8,128)S(1)}, f32[128,256]{1,0:T(8,128)S(1)}, f32[128,256]{1,0:T(8,128)S(1)}, f32[6...) custom-call(bf16[32,256,256]{2,1,0:T(8,128)(2,1)S(1)} %get-tuple-element.32.enc, ...), custom_call_target="tpu_custom_call" | custom-call | tf_op jit(solution)/shard_map/sage/pallas_call | solution.py:858
  43.2 0.0 copy-start
  43.3 0.0 copy-start.1
  43.3 0.0 copy-start.2
  43.3 0.0 copy-start.3
  43.3 4.2 %backward.1 = (f32[128,256]{1,0:T(8,128)S(1)}, f32[128,128]{1,0:T(8,128)S(1)}) custom-call(s32[8,256]{1,0:T(8,128)S(4)} %get-tuple-element.30.lists, bf16[192,256,256]{2,1,0:T(8,128)(2,1)S(1)} %get-tuple-element.31.tiles, bf16[32,128,256]{2,1,0:T(8,128)(2,1)S(1)} %get-tuple-element.37.sums, f32[16,128,256]{2,1,0:T(8,128)S(1)} %get-tuple-element.38.self_back, ...), custom_call_target="tpu_custom_call" | custom-call | tf_op jit(solution)/shard_map/backward/pallas_call | solution.py:882
  47.5 13.7 %reduce.1 = (f32[80,128]{1,0:T(8,128)S(1)}, f32[8,128]{1,0:T(8,128)S(1)}) custom-call(f32[128,256]{1,0:T(8,128)S(1)} %get-tuple-element.40.enc_grad, f32[128,128]{1,0:T(8,128)S(1)} %get-tuple-element.41.benc_grad, f32[128,256]{1,0:T(8,128)S(1)} %get-tuple-element.42.self_grad, f32[128,256]{1,0:T(8,128)S(1)} %get-tuple-element.43.neigh_grad, ...), custom_call_target="tpu_custom_call" | custom-call | tf_op jit(solution)/shard_map/reduce/pallas_call | solution.py:892
  61.2 0.0 copy-done
  61.2 0.0 copy-done.1
  61.2 0.0 copy-done.2
  61.3 0.0 copy-done.3
  61.3 0.8 %update.1 = (f32[2,64,79]{2,1,0:T(8,128)}, f32[2,64,79]{2,1,0:T(8,128)}, f32[2,64,79]{2,1,0:T(8,128)}, bf16[2,64,79]{2,1,0:T(8,128)(2,1)}, f32[1,1]{1,0:T(1,128)}) custom-call(f32[80,128]{1,0:T(8,128)S(1)} %get-tuple-element.48.packed, f32[8,128]{1,0:T(8,128)S(1)} %get-tuple-element.49.loss, s32[8,79]{1,0:T(8,128)S(1)} %copy-done.3, ...), custom_call_target="tpu_custom_call" | custom-call | tf_op jit(solution)/shard_map/update/pallas_call | solution.py:919
Async XLA Ops:
  43.2 18.0 %copy-start = (f32[79,2,64]{0,2,1:T(8,128)S(1)}, f32[79,2,64]{0,2,1:T(8,128)}, u32[]{:S(2)}) copy-start(f32[79,2,64]{0,2,1:T(8,128)} %param.19) | copy-start | bytes 121348
  43.3 18.0 %copy-start.1 = (f32[79,2,64]{0,2,1:T(8,128)S(1)}, f32[79,2,64]{0,2,1:T(8,128)}, u32[]{:S(2)}) copy-start(f32[79,2,64]{0,2,1:T(8,128)} %param.20) | copy-start | bytes 121348
  43.3 18.0 %copy-start.2 = (f32[79,2,64]{0,2,1:T(8,128)S(1)}, f32[79,2,64]{0,2,1:T(8,128)}, u32[]{:S(2)}) copy-start(f32[79,2,64]{0,2,1:T(8,128)} %param.21) | copy-start | bytes 121348
  43.3 18.0 %copy-start.3 = (s32[8,79]{1,0:T(8,128)S(1)}, s32[8,79]{1,0:T(8,128)}, u32[]{:S(2)}) copy-start(s32[8,79]{1,0:T(8,128)} %pieces.3) | copy-start | bytes 7588

commit v5 on v4

--- a/solution.py
+++ b/solution.py
@@ -272,8 +272,9 @@
 
     fmine, frow = split(rvec)
     bmine, bcol = split(cvec)
-    fmine = fmine & live
-    bmine = bmine & live
+    diagonal = fmine & live & (rvec == cvec)
+    fmine = fmine & live & (rvec != cvec)
+    bmine = bmine & live & (rvec != cvec)
     upto = (
         lax.broadcasted_iota(jnp.int32, (tpad, tpad), 0)
         <= lax.broadcasted_iota(jnp.int32, (tpad, tpad), 1)
@@ -294,7 +295,11 @@
 
     ft, fr, fc, fn = compact(fmine, frow, cvec)
     bt, bc, br, bn = compact(bmine, bcol, rvec)
-    lbuf[...] = jnp.concatenate([ft, fr, fc, bt, bc, br, fn, bn], axis=0)
+    chosen = (order == jnp.where(diagonal, frow, -1)).astype(f32).astype(bf16)
+    index = jnp.broadcast_to(tvec.astype(f32), (8, tpad)).astype(bf16)
+    first_tile = dot_nt(index, chosen)[0:1].astype(jnp.int32)
+    counts = jnp.where(tvec == 0, fn, bn)
+    lbuf[...] = jnp.concatenate([ft, fr, fc, bt, bc, br, counts, first_tile], axis=0)
     put = pltpu.make_async_copy(lbuf, lists, put_sem)
     put.start()
     inverse[...] = 1.0 / deg[...].astype(f32)
@@ -397,21 +402,34 @@
 
 
 def each_tile(count, use):
-    def many(i, c):
+    done = 0
+
+    def step0(i, c, start=done):
         for u in range(32):
-            use(i * 32 + u)
-        return c
-
-    whole = count // 32
-    lax.fori_loop(0, whole, many, 0)
-    done = whole * 32
-
-    def few(i, c):
+            use(start + i * 32 + u)
+        return c
+
+    trips0 = (count - done) // 32
+    lax.fori_loop(0, trips0, step0, 0)
+    done = done + trips0 * 32
+
+    def step1(i, c, start=done):
+        for u in range(16):
+            use(start + i * 16 + u)
+        return c
+
+    trips1 = (count - done) // 16
+    lax.fori_loop(0, trips1, step1, 0)
+    done = done + trips1 * 16
+
+    def step2(i, c, start=done):
         for u in range(8):
-            use(done + i * 8 + u)
-        return c
-
-    lax.fori_loop(0, (count - done + 7) // 8, few, 0)
+            use(start + i * 8 + u)
+        return c
+
+    trips2 = (count - done + 7) // 8
+    lax.fori_loop(0, trips2, step2, 0)
+    done = done + trips2 * 8
 
 
 def forward_kernel(lists, tiles, enc, inverse, mean, acc):
@@ -421,11 +439,10 @@
     def use(j):
         acc[lists[1, j]] += dot_nt(enc[lists[2, j]], tiles[lists[0, j]])
 
-    def clear(i, c):
-        acc[i] = jnp.zeros((B, B), f32)
-        return c
-
-    lax.fori_loop(0, local + 1, clear, 0)
+    k = lax.axis_index("col") % 2
+    for i in range(local):
+        at = (i // blocks) * 2 * blocks + k * blocks + i % blocks
+        acc[i] = dot_nt(enc[at], tiles[lists[7, i]])
     each_tile(lists[6, 0], use)
 
     def finish(i, c):
@@ -569,12 +586,11 @@
     def use(j):
         acc[lists[4, j]] += dot_nn(sums[lists[5, j]], tiles[lists[3, j]])
 
-    def clear(i, c):
-        acc[i] = jnp.zeros((HALF, B), f32)
-        return c
-
-    lax.fori_loop(0, local + 1, clear, 0)
-    each_tile(lists[7, 0], use)
+    k = lax.axis_index("col") % 2
+    for i in range(local):
+        at = (i // blocks) * 2 * blocks + k * blocks + i % blocks
+        acc[i] = dot_nn(sums[at], tiles[lists[7, i]])
+    each_tile(lists[6, 1], use)
     half = pl.ds(pl.multiple_of(x * HALF, HALF), HALF)
     wide = column_of(table[PROWS - 2 : PROWS + 14, half], 0)
     wide = jnp.concatenate([wide, wide], axis=1)

time: 61.8 us -> 61 us (0.987)
  Pallas kernels: 60.7 us -> 59.4 us
    pallas_call x1, Pallas kernels: 4.44 us -> 3.29 us  [body(): pl.pallas_call(forward_kernel, out_shape=pltpu.VMEM((local, HID, B), bf16...]
where the time goes in v5:
time: 61 us
  Pallas kernels  59.4 us (97%)
  between operations  1.54 us (3%)
    pallas_call x1, Pallas kernels, body(): pl.pallas_call(functools.partial(gather_kernel, ng), out_shape=(pltpu.VME...  30.4 us
    pallas_call x1, Pallas kernels, body(): pl.pallas_call(functools.partial(reduce_kernel, ng), out_shape=(pltpu.VME...  14.2 us
    pallas_call x1, Pallas kernels, body(): pl.pallas_call(sage_kernel, out_shape=(pltpu.VMEM((nb, HALF, B), bf16), p...  7.06 us
    pallas_call x1, Pallas kernels, body(): pl.pallas_call(backward_kernel, out_shape=(pltpu.VMEM((HALF, F), f32), pl...  3.62 us
    pallas_call x1, Pallas kernels, body(): pl.pallas_call(forward_kernel, out_shape=pltpu.VMEM((local, HID, B), bf16...  3.29 us

profile of v5, /device:TPU:0, one launch (start us, length us, event | category | flops | bytes accessed | tf_op | source)
XLA Modules:
  0.0 61.0 jit_solution(15750511728587085019)
XLA Ops:
  1.3 30.4 %gather.1 = (bf16[192,256,256]{2,1,0:T(8,128)(2,1)S(1)}, bf16[2,2048,256]{2,1,0:T(8,128)(2,1)S(1)}, bf16[32,256,256]{2,1,0:T(8,128)(2,1)S(1)}, bf16[848,256]{1,0...) custom-call(bf16[2048,256]{1,0:T(8,128)(2,1)} %feat.1, ...), custom_call_target="tpu_custom_call" | custom-call | tf_op jit(solution)/shard_map/gather/pallas_call | solution.py:805
  31.7 3.3 %forward.1.mean = bf16[16,256,256]{2,1,0:T(8,128)(2,1)S(1)} custom-call(s32[8,256]{1,0:T(8,128)S(4)} %get-tuple-element.30.lists, bf16[192,256,256]{2,1,0:T(8,128)(2,1)S(1)} %get-tuple-element.31.tiles, bf16[32,256,256]{2,1,0:T(8,128)(2,1)S(1)} %get-tuple-element.32.enc, f32[2,1,2048]{2,1,0:T(1,128)S(1)} %get-tuple-element.33.inverse), custom_call_target="tpu_custom_call" | custom-call | tf_op jit(solution)/shard_map/forward/pallas_call | solution.py:864
  35.0 7.1 %sage.1 = (bf16[32,128,256]{2,1,0:T(8,128)(2,1)S(1)}, f32[16,128,256]{2,1,0:T(8,128)S(1)}, f32[128,256]{1,0:T(8,128)S(1)}, f32[128,256]{1,0:T(8,128)S(1)}, f32[6...) custom-call(bf16[32,256,256]{2,1,0:T(8,128)(2,1)S(1)} %get-tuple-element.32.enc, ...), custom_call_target="tpu_custom_call" | custom-call | tf_op jit(solution)/shard_map/sage/pallas_call | solution.py:874
  42.1 0.0 copy-start
  42.1 0.0 copy-start.1
  42.1 0.0 copy-start.2
  42.1 0.0 copy-start.3
  42.2 3.6 %backward.1 = (f32[128,256]{1,0:T(8,128)S(1)}, f32[128,128]{1,0:T(8,128)S(1)}) custom-call(s32[8,256]{1,0:T(8,128)S(4)} %get-tuple-element.30.lists, bf16[192,256,256]{2,1,0:T(8,128)(2,1)S(1)} %get-tuple-element.31.tiles, bf16[32,128,256]{2,1,0:T(8,128)(2,1)S(1)} %get-tuple-element.37.sums, f32[16,128,256]{2,1,0:T(8,128)S(1)} %get-tuple-element.38.self_back, ...), custom_call_target="tpu_custom_call" | custom-call | tf_op jit(solution)/shard_map/backward/pallas_call | solution.py:898
  45.8 14.2 %reduce.1 = (f32[80,128]{1,0:T(8,128)S(1)}, f32[8,128]{1,0:T(8,128)S(1)}) custom-call(f32[128,256]{1,0:T(8,128)S(1)} %get-tuple-element.40.enc_grad, f32[128,128]{1,0:T(8,128)S(1)} %get-tuple-element.41.benc_grad, f32[128,256]{1,0:T(8,128)S(1)} %get-tuple-element.42.self_grad, f32[128,256]{1,0:T(8,128)S(1)} %get-tuple-element.43.neigh_grad, ...), custom_call_target="tpu_custom_call" | custom-call | tf_op jit(solution)/shard_map/reduce/pallas_call | solution.py:908
  60.0 0.0 copy-done
  60.0 0.0 copy-done.1
  60.0 0.0 copy-done.2
  60.0 0.0 copy-done.3
  60.0 0.8 %update.1 = (f32[2,64,79]{2,1,0:T(8,128)}, f32[2,64,79]{2,1,0:T(8,128)}, f32[2,64,79]{2,1,0:T(8,128)}, bf16[2,64,79]{2,1,0:T(8,128)(2,1)}, f32[1,1]{1,0:T(1,128)}) custom-call(f32[80,128]{1,0:T(8,128)S(1)} %get-tuple-element.48.packed, f32[8,128]{1,0:T(8,128)S(1)} %get-tuple-element.49.loss, s32[8,79]{1,0:T(8,128)S(1)} %copy-done.3, ...), custom_call_target="tpu_custom_call" | custom-call | tf_op jit(solution)/shard_map/update/pallas_call | solution.py:935
Async XLA Ops:
  42.1 17.9 %copy-start = (f32[79,2,64]{0,2,1:T(8,128)S(1)}, f32[79,2,64]{0,2,1:T(8,128)}, u32[]{:S(2)}) copy-start(f32[79,2,64]{0,2,1:T(8,128)} %param.19) | copy-start | bytes 121348
  42.1 17.9 %copy-start.1 = (f32[79,2,64]{0,2,1:T(8,128)S(1)}, f32[79,2,64]{0,2,1:T(8,128)}, u32[]{:S(2)}) copy-start(f32[79,2,64]{0,2,1:T(8,128)} %param.20) | copy-start | bytes 121348
  42.1 17.9 %copy-start.2 = (f32[79,2,64]{0,2,1:T(8,128)S(1)}, f32[79,2,64]{0,2,1:T(8,128)}, u32[]{:S(2)}) copy-start(f32[79,2,64]{0,2,1:T(8,128)} %param.21) | copy-start | bytes 121348
  42.1 17.9 %copy-start.3 = (s32[8,79]{1,0:T(8,128)S(1)}, s32[8,79]{1,0:T(8,128)}, u32[]{:S(2)}) copy-start(s32[8,79]{1,0:T(8,128)} %pieces.3) | copy-start | bytes 7588

commit v6 on v5

--- a/solution.py
+++ b/solution.py
@@ -697,8 +697,8 @@
         src = (g + ng - d) % ng
         return remote(qbuf.at[src], inbox.at[src], g_send.at[d], g_recv.at[d], (src, q))
 
-    def start(d, c):
-        out(d).start()
+    def start(i, c):
+        out(ng // 2 + (i // 2) * (1 - 2 * (i % 2))).start()
         return c
 
     lax.fori_loop(1, ng, start, 0)

time: 61 us -> 62.4 us (1.023)
  Pallas kernels: 59.4 us -> 61 us
    pallas_call x1, Pallas kernels: 14.2 us -> 12.4 us  [body(): pl.pallas_call(functools.partial(reduce_kernel, ng), out_shape=(pltpu.VME...]
    pallas_call x1, Pallas kernels: 3.29 us -> 4.88 us  [body(): pl.pallas_call(forward_kernel, out_shape=pltpu.VMEM((local, HID, B), bf16...]
    pallas_call x1, Pallas kernels: 3.62 us -> 4.52 us  [body(): pl.pallas_call(backward_kernel, out_shape=(pltpu.VMEM((HALF, F), f32), pl...]
    pallas_call x1, Pallas kernels: 7.06 us -> 7.94 us  [body(): pl.pallas_call(sage_kernel, out_shape=(pltpu.VMEM((nb, HALF, B), bf16), p...]
where the time goes in v6:
time: 62.4 us; the launch traced here: 62.5 us
  Pallas kernels  61 us (98%)
  between operations  1.54 us (2%)
    pallas_call x1, Pallas kernels, body(): pl.pallas_call(functools.partial(gather_kernel, ng), out_shape=(pltpu.VME...  30.4 us
    pallas_call x1, Pallas kernels, body(): pl.pallas_call(functools.partial(reduce_kernel, ng), out_shape=(pltpu.VME...  12.4 us
    pallas_call x1, Pallas kernels, body(): pl.pallas_call(sage_kernel, out_shape=(pltpu.VMEM((nb, HALF, B), bf16), p...  7.94 us
    pallas_call x1, Pallas kernels, body(): pl.pallas_call(forward_kernel, out_shape=pltpu.VMEM((local, HID, B), bf16...  4.88 us
    pallas_call x1, Pallas kernels, body(): pl.pallas_call(backward_kernel, out_shape=(pltpu.VMEM((HALF, F), f32), pl...  4.52 us

profile of v6, /device:TPU:0, one launch (start us, length us, event | category | flops | bytes accessed | tf_op | source)
XLA Modules:
  0.0 62.5 jit_solution(11277912534803369858)
XLA Ops:
  1.3 30.4 %gather.1 = (bf16[192,256,256]{2,1,0:T(8,128)(2,1)S(1)}, bf16[2,2048,256]{2,1,0:T(8,128)(2,1)S(1)}, bf16[32,256,256]{2,1,0:T(8,128)(2,1)S(1)}, bf16[848,256]{1,0...) custom-call(bf16[2048,256]{1,0:T(8,128)(2,1)} %feat.1, ...), custom_call_target="tpu_custom_call" | custom-call | tf_op jit(solution)/shard_map/gather/pallas_call | solution.py:805
  31.7 4.9 %forward.1.mean = bf16[16,256,256]{2,1,0:T(8,128)(2,1)S(1)} custom-call(s32[8,256]{1,0:T(8,128)S(4)} %get-tuple-element.30.lists, bf16[192,256,256]{2,1,0:T(8,128)(2,1)S(1)} %get-tuple-element.31.tiles, bf16[32,256,256]{2,1,0:T(8,128)(2,1)S(1)} %get-tuple-element.32.enc, f32[2,1,2048]{2,1,0:T(1,128)S(1)} %get-tuple-element.33.inverse), custom_call_target="tpu_custom_call" | custom-call | tf_op jit(solution)/shard_map/forward/pallas_call | solution.py:864
  36.6 7.9 %sage.1 = (bf16[32,128,256]{2,1,0:T(8,128)(2,1)S(1)}, f32[16,128,256]{2,1,0:T(8,128)S(1)}, f32[128,256]{1,0:T(8,128)S(1)}, f32[128,256]{1,0:T(8,128)S(1)}, f32[6...) custom-call(bf16[32,256,256]{2,1,0:T(8,128)(2,1)S(1)} %get-tuple-element.32.enc, ...), custom_call_target="tpu_custom_call" | custom-call | tf_op jit(solution)/shard_map/sage/pallas_call | solution.py:874
  44.6 0.0 copy-start
  44.6 0.0 copy-start.1
  44.6 0.0 copy-start.2
  44.6 0.0 copy-start.3
  44.6 4.5 %backward.1 = (f32[128,256]{1,0:T(8,128)S(1)}, f32[128,128]{1,0:T(8,128)S(1)}) custom-call(s32[8,256]{1,0:T(8,128)S(4)} %get-tuple-element.30.lists, bf16[192,256,256]{2,1,0:T(8,128)(2,1)S(1)} %get-tuple-element.31.tiles, bf16[32,128,256]{2,1,0:T(8,128)(2,1)S(1)} %get-tuple-element.37.sums, f32[16,128,256]{2,1,0:T(8,128)S(1)} %get-tuple-element.38.self_back, ...), custom_call_target="tpu_custom_call" | custom-call | tf_op jit(solution)/shard_map/backward/pallas_call | solution.py:898
  49.1 12.4 %reduce.1 = (f32[80,128]{1,0:T(8,128)S(1)}, f32[8,128]{1,0:T(8,128)S(1)}) custom-call(f32[128,256]{1,0:T(8,128)S(1)} %get-tuple-element.40.enc_grad, f32[128,128]{1,0:T(8,128)S(1)} %get-tuple-element.41.benc_grad, f32[128,256]{1,0:T(8,128)S(1)} %get-tuple-element.42.self_grad, f32[128,256]{1,0:T(8,128)S(1)} %get-tuple-element.43.neigh_grad, ...), custom_call_target="tpu_custom_call" | custom-call | tf_op jit(solution)/shard_map/reduce/pallas_call | solution.py:908
  61.5 0.0 copy-done
  61.5 0.0 copy-done.1
  61.5 0.0 copy-done.2
  61.5 0.0 copy-done.3
  61.5 0.8 %update.1 = (f32[2,64,79]{2,1,0:T(8,128)}, f32[2,64,79]{2,1,0:T(8,128)}, f32[2,64,79]{2,1,0:T(8,128)}, bf16[2,64,79]{2,1,0:T(8,128)(2,1)}, f32[1,1]{1,0:T(1,128)}) custom-call(f32[80,128]{1,0:T(8,128)S(1)} %get-tuple-element.48.packed, f32[8,128]{1,0:T(8,128)S(1)} %get-tuple-element.49.loss, s32[8,79]{1,0:T(8,128)S(1)} %copy-done.3, ...), custom_call_target="tpu_custom_call" | custom-call | tf_op jit(solution)/shard_map/update/pallas_call | solution.py:935
Async XLA Ops:
  44.6 16.9 %copy-start = (f32[79,2,64]{0,2,1:T(8,128)S(1)}, f32[79,2,64]{0,2,1:T(8,128)}, u32[]{:S(2)}) copy-start(f32[79,2,64]{0,2,1:T(8,128)} %param.19) | copy-start | bytes 121348
  44.6 16.9 %copy-start.1 = (f32[79,2,64]{0,2,1:T(8,128)S(1)}, f32[79,2,64]{0,2,1:T(8,128)}, u32[]{:S(2)}) copy-start(f32[79,2,64]{0,2,1:T(8,128)} %param.20) | copy-start | bytes 121348
  44.6 16.9 %copy-start.2 = (f32[79,2,64]{0,2,1:T(8,128)S(1)}, f32[79,2,64]{0,2,1:T(8,128)}, u32[]{:S(2)}) copy-start(f32[79,2,64]{0,2,1:T(8,128)} %param.21) | copy-start | bytes 121348
  44.6 16.9 %copy-start.3 = (s32[8,79]{1,0:T(8,128)S(1)}, s32[8,79]{1,0:T(8,128)}, u32[]{:S(2)}) copy-start(s32[8,79]{1,0:T(8,128)} %pieces.3) | copy-start | bytes 7588
